TPU v7x, 256 devices: a whole 4x4x8 slice. The times are simulated.
256 devices in a mesh: seq: 32 (over y, z), head: 8 (over x, core).
Axes of the slice: x: 4, y: 4, z: 8, core: 2. Of those that a mesh axis runs over, the one named last changes fastest.
Arguments:
- query_rows: bfloat16 [32768, 4096], P('seq', 'head'), may hold values from -6 to 6
- key_rows: bfloat16 [32768, 4096], P('seq', 'head'), may hold values from -6 to 6
- value_rows: bfloat16 [32768, 4096], P('seq', 'head'), may hold values from -15 to 15
- block_picks: int32 [64, 32, 4], P('seq', 'head'), may hold values from -1 to 63, as said below
- out_weight: bfloat16 [4096, 4096], P(None, 'head'), may hold values from -0.09375 to 0.09375
Outputs:
- mixed: bfloat16 [32768, 4096], P('seq', 'head')
Inputs may be any that keep to these rules, and one draw needn't show every extreme that they name: `block_picks`: every entry that is not -1 names a block held by a lower index of seq than block b. Repeated entries of one row count once. Over the query blocks of one index of seq and the heads of one index of head, at most 2 entries name blocks of any one other index of seq, and every index of seq from 1 on has exactly 2 entries naming blocks of index 0.
All inputs are finite; a program needn't handle non-finite values.
Results may differ from a plain program's by a relative error of at most 0.0059.
Values may be sent and summed in bfloat16 or wider, within the bound.
A program may use at most 192 MiB of HBM per device.

v0:
```python
import jax
import jax.numpy as jnp
from jax import lax
from jax.sharding import Mesh
from jax.sharding import PartitionSpec as P

CAP = 2
SEQ = ("seq_0", "seq_1")


def joined_along(tiles, dim):
    tiles = jnp.moveaxis(tiles, 0, dim)
    shape = tiles.shape
    return tiles.reshape(*shape[:dim], shape[dim] * shape[dim + 1], *shape[dim + 2 :])


def all_blocks(shard, axes, order):
    tiles = shard
    for k in order:
        tiles = lax.all_gather(tiles, axes[k])
    done = order[::-1]
    back = [done.index(k) for k in range(len(axes))]
    tiles = tiles.transpose(*back, *range(len(axes), tiles.ndim))
    return tiles.reshape(-1, *shard.shape)


def gather_axes(shard, axes, order, dim):
    return joined_along(all_blocks(shard, axes, order), dim)


def tile_partial(query_tile, key_tile, value_tile, causal_mask):
    score_scale = query_tile.shape[-1] ** (-0.5)
    scores = (
        jnp.einsum("nqd,nkd->nqk", query_tile, key_tile, preferred_element_type=jnp.float32)
        * score_scale
    )
    if causal_mask is not None:
        scores = jnp.where(causal_mask, scores, -jnp.inf)
    maxima = jnp.max(scores, axis=-1)
    shifted = jnp.exp(scores - maxima[..., None])
    totals = jnp.sum(shifted, axis=-1)
    weights = shifted.astype(jnp.bfloat16)
    partial_out = jnp.einsum(
        "nqk,nkd->nqd", weights, value_tile, preferred_element_type=jnp.float32
    )
    return (partial_out.astype(jnp.bfloat16), maxima, totals)


def grouped_partial(query_tile, key_tile, value_tile):
    tile_count = query_tile.shape[0]
    groups = 1
    while tile_count % (groups * 2) == 0 and tile_count // groups > 16:
        groups = groups * 2

    def one_group(operands):
        return tile_partial(operands[0], operands[1], operands[2], None)

    reshaped = tuple(
        (
            operand.reshape((groups, tile_count // groups) + operand.shape[1:])
            for operand in (query_tile, key_tile, value_tile)
        )
    )
    results = lax.map(one_group, reshaped)
    return tuple(
        (result_array.reshape((tile_count,) + result_array.shape[2:]) for result_array in results)
    )


def plan_slots(picks_local, per_device, seq_count, capacity):
    blocks_here, heads_here, pick_count = picks_local.shape
    usable_cols = []
    for column in range(pick_count):
        entries = picks_local[:, :, column]
        is_fresh = entries >= 0
        for earlier in range(column):
            is_fresh = is_fresh & (entries != picks_local[:, :, earlier])
        usable_cols.append(is_fresh)
    usable = jnp.stack(usable_cols, 2).reshape(-1)
    flat_picks = picks_local.reshape(-1)
    owner_dev = jnp.where(usable, flat_picks // per_device, -1)
    onehot = (owner_dev[:, None] == jnp.arange(seq_count, dtype=jnp.int32)[None, :]).astype(
        jnp.int32
    )
    before = jnp.cumsum(onehot, axis=0) - onehot
    bucket_rank = jnp.sum(before * onehot, axis=1)
    slot_index = jnp.where(usable, owner_dev * capacity + bucket_rank, -1)
    entry_ids = jnp.arange(flat_picks.shape[0], dtype=jnp.int32)
    head_of = entry_ids // pick_count % heads_here
    tile_code = jnp.maximum(flat_picks, 0) % per_device * heads_here + head_of
    matches = slot_index[:, None] == jnp.arange(seq_count * capacity, dtype=jnp.int32)[None, :]
    request_table = jnp.sum(jnp.where(matches, tile_code[:, None] + 1, 0), axis=0) - 1
    sender = jnp.sum(jnp.where(matches, entry_ids[:, None], 0), axis=0)
    return (usable, jnp.maximum(slot_index, 0), request_table.reshape(seq_count, capacity), sender)


def body(query_rows, key_rows, value_rows, block_picks, out_weight):
    seq_count = lax.axis_size(SEQ)
    my_index = lax.axis_index(SEQ)
    capacity = CAP
    tok_rows, feature_width = query_rows.shape
    blocks_here, heads_here, pick_count = block_picks.shape
    block_rows = tok_rows // blocks_here
    head_width = feature_width // heads_here
    pair_count = blocks_here * heads_here

    def by_head(rows_in):
        shaped = rows_in.reshape(blocks_here, block_rows, heads_here, head_width)
        return jnp.transpose(shaped, (0, 2, 1, 3)).reshape(pair_count, block_rows, head_width)

    query_tiles = by_head(query_rows)
    key_tiles = by_head(key_rows)
    value_tiles = by_head(value_rows)
    positions = jnp.arange(block_rows)
    causal_mask = (positions[:, None] >= positions[None, :])[None]
    own_out, own_max, own_total = tile_partial(query_tiles, key_tiles, value_tiles, causal_mask)
    usable, slot_index, request_table, sender = plan_slots(
        block_picks, blocks_here, seq_count, capacity
    )
    everyone = gather_axes(block_picks, SEQ, (0, 1), 0)
    everyone = everyone.reshape((seq_count, blocks_here, heads_here, pick_count))
    tables = jax.vmap(lambda picks_one: plan_slots(picks_one, blocks_here, seq_count, capacity)[2])(
        everyone
    )
    incoming = lax.dynamic_index_in_dim(tables, my_index, 1, keepdims=False)
    wanted = jnp.maximum(incoming, 0).reshape(-1)
    asking = jnp.broadcast_to(
        query_tiles[:, None], (pair_count, pick_count, block_rows, head_width)
    )
    asking = asking.reshape(pair_count * pick_count, block_rows, head_width)
    stacked = jnp.stack((key_tiles, value_tiles), 1)
    outgoing = stacked[wanted].reshape((seq_count, capacity) + stacked.shape[1:])
    arrived = lax.all_to_all(outgoing, SEQ, split_axis=0, concat_axis=0, tiled=True)
    arrived = arrived.reshape((seq_count * capacity,) + stacked.shape[1:])[slot_index]
    far_out, far_max, far_total = grouped_partial(asking, arrived[:, 0], arrived[:, 1])
    all_out = jnp.concatenate(
        [own_out[:, None], far_out.reshape(pair_count, pick_count, block_rows, head_width)], 1
    )
    all_max = jnp.concatenate(
        [own_max[:, None], far_max.reshape(pair_count, pick_count, block_rows)], 1
    )
    all_total = jnp.concatenate(
        [own_total[:, None], far_total.reshape(pair_count, pick_count, block_rows)], 1
    )
    all_usable = jnp.concatenate(
        [jnp.ones((pair_count, 1), dtype=jnp.bool_), usable.reshape(pair_count, pick_count)], 1
    )
    keep = all_usable[:, :, None]
    largest = jnp.max(jnp.where(keep, all_max, -jnp.inf), axis=1)
    factor = jnp.where(keep, jnp.exp(all_max - largest[:, None]), 0.0)
    numer = jnp.sum(factor[..., None] * all_out.astype(jnp.float32), axis=1)
    denom = jnp.sum(factor * all_total, axis=1)
    combined = (numer / denom[..., None]).astype(jnp.bfloat16)
    combined = combined.reshape(blocks_here, heads_here, block_rows, head_width)
    attended = jnp.transpose(combined, (0, 2, 1, 3)).reshape(tok_rows, feature_width)
    mixed = jnp.dot(
        lax.all_gather(attended, "head", axis=1, tiled=True),
        out_weight,
        preferred_element_type=jnp.float32,
    )
    return mixed.astype(jnp.bfloat16)


def solution(mesh):
    finer = Mesh(mesh.devices.reshape(4, 8, mesh.shape["head"]), ("seq_0", "seq_1", "head"))
    return jax.shard_map(
        body,
        mesh=finer,
        in_specs=(
            P(SEQ, "head"),
            P(SEQ, "head"),
            P(SEQ, "head"),
            P(SEQ, "head", None),
            P(None, "head"),
        ),
        out_specs=P(SEQ, "head"),
        check_vma=False,
    )
```

profile of v0, /device:TPU:104, one launch (start us, length us, event | category | flops | bytes accessed | tf_op | source)
XLA Modules:
  0.0 599.5 jit_solution(16996632091065717557)
XLA Ops:
  6.5 12.4 %all-gather = s32[8,4,4]{2,1,0:T(4,128)S(1)} all-gather(s32[2,4,4]{2,1,0:T(4,128)} %param.10), channel_id=2, replica_groups=mesh['seq_0'=4,'seq_1'=8,'head'=8] {'seq_0'}, dimensions={0}, use_global_device_ids=true | all-gather | bytes 640 | tf_op jit(solution)/shard_map/all_gather | solution.py:20
  18.9 25.5 %all-gather.1 = s32[32,2,4,4]{3,1,0,2:T(2,128)S(1)} all-gather(s32[4,2,4,4]{3,1,0,2:T(2,128)S(1)} %bitcast.107), channel_id=3, replica_groups=mesh['seq_0'=4,'seq_1'=8,'head'=8] {'seq_1'}, dimensions={0}, use_global_device_ids=true | all-gather | bytes 4608 | tf_op jit(solution)/shard_map/all_gather | solution.py:20
  44.4 0.3 copy.151
  45.5 1.0 fusion.67
  46.6 0.4 select_reduce_fusion
  47.3 1.3 reshape.323
  48.8 1.3 reshape.325
  50.3 1.0 copy-done
  51.5 7.4 %gather_fusion = bf16[64,2,512,128]{3,2,1,0:T(8,128)(2,1)} fusion(bf16[8,2,512,128]{3,2,0,1:T(8,128)(2,1)S(1)} %pad_maximum_fusion, s32[1024]{0:T(1024)S(1)} %pad_clamp_fusion.1), kind=kCustom, calls=%fused_computation | custom fusion | bytes 33554688 | tf_op jit(solution)/shard_map/gather | solution.py:132
  58.9 9.0 %all-to-all-start = ((bf16[32,2,2,512,128]{4,3,2,1,0:T(8,128)(2,1)}), bf16[32,2,2,512,128]{4,3,2,1,0:T(8,128)(2,1)}, u32[]{:S(2)}, u32[]{:S(2)}) async-start(bf16[32,2,2,512,128]{4,3,2,1,0:T(8,128)(2,1)} %bitcast.85), calls=%async_computation | async-start | bytes 33554432 | tf_op jit(solution)/shard_map/all_to_all | solution.py:133
  69.0 0.3 reshape.321
  70.0 1.4 fusion.21
  71.4 1.7 fusion.22
  73.5 2.5 fusion.33
  76.0 356.7 %all-to-all-done = bf16[32,2,2,512,128]{4,3,2,1,0:T(8,128)(2,1)} async-done(((bf16[32,2,2,512,128]{4,3,2,1,0:T(8,128)(2,1)}), bf16[32,2,2,512,128]{4,3,2,1,0:T(8,128)(2,1)}, u32[]{:S(2)}, u32[]{:S(2)}) %all-to-all-start) | async-done | bytes 16777248 | tf_op jit(solution)/shard_map/all_to_all | solution.py:133
  432.7 10.7 %gather_fusion.1 = bf16[32,2,512,128]{3,2,1,0:T(8,128)(2,1)} fusion(bf16[64,2,512,128]{3,2,1,0:T(8,128)(2,1)} %bitcast.22, s32[1024]{0:T(1024)S(1)} %pad_clamp_fusion), kind=kCustom, calls=%fused_computation.1 | custom fusion | bytes 16777344 | tf_op jit(solution)/shard_map/gather | solution.py:134
  443.5 5.9 fusion.66
  449.4 3.0 broadcast_in_dim.97
  452.4 60.3 %while.14 = (s32[]{:T(128)}, bf16[2,16,512,128]{3,2,1,0:T(8,128)(2,1)}, f32[2,16,512]{2,1,0:T(8,128)S(1)}, f32[2,16,512]{2,1,0:T(8,128)S(1)}, bf16[2,16,512,128]...) while((s32[]{:T(128)}, ...), condition=%wide.region_9.10_spmd, body=%wide.region_6.9_spmd.sunk | while | flops 2182070272 | bytes 58984536 | solution.py:64
  452.4 10.3 %multiply_reduce_fusion.3 = (f32[16,512]{1,0:T(8,128)S(1)}, f32[16,512,512]{1,2,0:T(8,128)}) fusion(bf16[2,16,512,128]{3,2,1,0:T(8,128)(2,1)} %get-tuple-element.163, s32[]{:T(128)} %get-tuple-element.150, bf16[2,16,512,128]{3,2,1,0:T(8,128)(2,1)} %get-tuple-element.162), kind=kOutput, calls=%fused_computation.3.clone.1 | convolution fusion | flops 1082122240 | bytes 21005312 | tf_op jit(solution)/shard_map/while/body/eval_jaxpr/nqd,nkd->nqk/dot_general | solution.py:34
  462.7 8.6 %fusion.78 = f32[16,512]{1,0:T(8,128)S(1)} fusion(f32[16,512,512]{1,2,0:T(8,128)} %get-tuple-element.138, f32[16,512]{1,0:T(8,128)S(1)} %get-tuple-element.139), kind=kLoop, calls=%fused_computation.4.clone.1 | loop fusion | flops 12574720 | bytes 16842752 | tf_op jit(solution)/shard_map/while/body/eval_jaxpr/reduce_sum | solution.py:41
  471.2 11.3 %bitcast_dynamic-update-slice_fusion.5 = bf16[2,16,512,128]{3,2,1,0:T(8,128)(2,1)} fusion(bf16[2,16,512,128]{3,2,1,0:T(8,128)(2,1)} %get-tuple-element.151, s32[]{:T(128)} %get-tuple-element.150, bf16[2,16,512,128]{3,2,1,0:T(8,128)(2,1)} %get-tuple-element.164, f32[16,512,512]{1,2,0:T(8,128)} %get-tuple-element.138, f32[16,512]{1,0:T(8,128)S(1)} %get-tuple-element.139), kind=kOutput, calls=%fused_computation.9.clone.1 | convolution fusion | flops 1087373312 | bytes 21005312 | tf_op jit(solution)/shard_map/while/body/eval_jaxpr/nqk,nkd->nqd/dot_general | solution.py:43
  482.5 10.3 %multiply_reduce_fusion.3 = (f32[16,512]{1,0:T(8,128)S(1)}, f32[16,512,512]{1,2,0:T(8,128)}) fusion(bf16[2,16,512,128]{3,2,1,0:T(8,128)(2,1)} %get-tuple-element.163, s32[]{:T(128)} %get-tuple-element.150, bf16[2,16,512,128]{3,2,1,0:T(8,128)(2,1)} %get-tuple-element.162), kind=kOutput, calls=%fused_computation.3.clone.1 | convolution fusion | flops 1082122240 | bytes 21005312 | tf_op jit(solution)/shard_map/while/body/eval_jaxpr/nqd,nkd->nqk/dot_general | solution.py:34
  492.8 8.6 %fusion.78 = f32[16,512]{1,0:T(8,128)S(1)} fusion(f32[16,512,512]{1,2,0:T(8,128)} %get-tuple-element.138, f32[16,512]{1,0:T(8,128)S(1)} %get-tuple-element.139), kind=kLoop, calls=%fused_computation.4.clone.1 | loop fusion | flops 12574720 | bytes 16842752 | tf_op jit(solution)/shard_map/while/body/eval_jaxpr/reduce_sum | solution.py:41
  501.4 11.3 %bitcast_dynamic-update-slice_fusion.5 = bf16[2,16,512,128]{3,2,1,0:T(8,128)(2,1)} fusion(bf16[2,16,512,128]{3,2,1,0:T(8,128)(2,1)} %get-tuple-element.151, s32[]{:T(128)} %get-tuple-element.150, bf16[2,16,512,128]{3,2,1,0:T(8,128)(2,1)} %get-tuple-element.164, f32[16,512,512]{1,2,0:T(8,128)} %get-tuple-element.138, f32[16,512]{1,0:T(8,128)S(1)} %get-tuple-element.139), kind=kOutput, calls=%fused_computation.9.clone.1 | convolution fusion | flops 1087373312 | bytes 21005312 | tf_op jit(solution)/shard_map/while/body/eval_jaxpr/nqk,nkd->nqd/dot_general | solution.py:43
  512.7 0.9 fusion.44
  513.6 6.5 %multiply_reduce_fusion.1 = f32[8,512,128]{2,1,0:T(8,128)S(1)} fusion(bf16[8,4,512,128]{3,2,1,0:T(8,128)(2,1)} %bitcast.93, bf16[8,1,512,128]{3,2,1,0:T(8,128)(2,1)S(1)} %fusion.33, f32[8,5,512]{2,1,0:T(8,128)S(1)} %get-tuple-element.90), kind=kLoop, calls=%fused_computation.23 | loop fusion | flops 9961472 | bytes 7421952 | tf_op jit(solution)/shard_map/reduce_sum | solution.py:151
  520.1 1.0 fusion.39
  521.1 0.8 copy.148
  521.9 1.2 copy.155
  523.1 59.5 %all-gather.4.cloned.1.call-done = bf16[1024,4096]{1,0:T(8,128)(2,1)} async-done(((bf16[1024,512]{1,0:T(8,128)(2,1)}), bf16[1024,4096]{1,0:T(8,128)(2,1)}) %all-gather.4.cloned.1.call-update) | async-done | bytes 8388624 | tf_op jit(solution)/shard_map/all_gather | solution.py:157
  582.6 10.0 %convolution_convert_fusion = bf16[1024,512]{1,0:T(8,128)(2,1)} fusion(bf16[1024,4096]{1,0:T(8,128)(2,1)} %all-gather.4.cloned.1.call-done, bf16[4096,512]{1,0:T(8,128)(2,1)} %param.11), kind=kOutput, calls=%fused_computation.36 | convolution fusion | flops 4295491584 | bytes 13631488 | tf_op jit(solution)/shard_map/dot_general | solution.py:156
  (63 shorter events, 3.8 us)
Async XLA Ops:
  50.3 1.0 copy-start
  58.9 9.3 %copy-start.3 = (s32[2,4,4]{2,1,0:T(4,128)S(1)}, s32[2,4,4]{2,1,0:T(4,128)}, u32[]{:S(2)}) copy-start(s32[2,4,4]{2,1,0:T(4,128)} %param.10) | copy-start | bytes 388
  58.9 10.1 %copy-start.2 = (bf16[1024,512]{1,0:T(8,128)(2,1)S(1)}, bf16[1024,512]{1,0:T(8,128)(2,1)}, u32[]{:S(2)}) copy-start(bf16[1024,512]{1,0:T(8,128)(2,1)} %param.7) | copy-start | bytes 3145732
  58.9 373.9 %all-to-all-start = ((bf16[32,2,2,512,128]{4,3,2,1,0:T(8,128)(2,1)}), bf16[32,2,2,512,128]{4,3,2,1,0:T(8,128)(2,1)}, u32[]{:S(2)}, u32[]{:S(2)}) async-start(bf16[32,2,2,512,128]{4,3,2,1,0:T(8,128)(2,1)} %bitcast.85), calls=%async_computation | async-start | bytes 33554432 | tf_op jit(solution)/shard_map/all_to_all | solution.py:133
  67.9 514.7 %all-gather.4.cloned.1.call-start = ((), (), s32[]{:S(2)}) async-start(), calls=%async_computation.1 | async-start | bytes 9437184 | tf_op jit(solution)/shard_map/all_gather | solution.py:157
  70.0 3.5 copy-start.1
Sparse Core Ops, SparseCore 0:
  523.2 59.3 all-gather.3
where the time goes:
time: 602 us; the launch traced here: 599 us
  waiting for transfers between devices  416 us (69%)
  matrix products  57.1 us (9%)
  blocking collectives  37.8 us (6%)
  local copies, waits for them, and re-layouts  35.7 us (6%)
  other arithmetic  29.6 us (5%)
  between operations  13.7 us (2%)
  starting transfers between devices  9.26 us (2%)
    all_to_all x1, waiting for transfers between devices, body(): lax.all_to_all(outgoing, SEQ, split_axis=0, concat_axis=0, tiled=True)  357 us
    all_gather x1, waiting for transfers between devices, body(): lax.all_gather(attended, 'head', axis=1, tiled=True)  59.5 us
    all_gather x2, blocking collectives, all_blocks(): tiles = lax.all_gather(tiles, axes[k])  37.8 us
    dot_general x3, matrix products, tile_partial(): jnp.einsum('nqk,nkd->nqd', weights, value_tile, preferred_element_type=jn...  25.1 us
    dot_general x3, matrix products, tile_partial(): jnp.einsum('nqd,nkd->nqk', query_tile, key_tile, preferred_element_type=j...  22 us
    reduce_sum x3, other arithmetic, tile_partial(): totals = jnp.sum(shifted, axis=-1)  18.8 us
  transfers between devices with their start and end apart: 2, of which 2 were waited for; matrix products, arithmetic and copies ran while one was open for 1% of the time, Pallas kernels for 0%

commit v1 on v0

v1 whole, which is shorter than its diff:
```python
import functools

import jax
import jax.numpy as jnp
from jax import lax
from jax.experimental import pallas as pl
from jax.experimental.pallas import tpu as pltpu
from jax.sharding import PartitionSpec as P

CAP = 2
RINGS = {32: (4, 8), 8: (2, 4), 4: (2, 2)}
LOG2E = 1.4426950408889634
MESH = pl.DeviceIdType.MESH


def plan_kernel(per_device, picks, asked, slot_of, meta, used, code):
    blocks, heads, columns = picks.shape
    owners = used.shape[0]

    def clear_owner(d, _):
        used[d] = 0
        return 0

    def clear_slot(i, _):
        asked[i] = 0
        code[i] = 0
        return 0

    lax.fori_loop(0, owners, clear_owner, 0)
    lax.fori_loop(0, owners * CAP, clear_slot, 0)

    def one_pair(pair, _):
        b, h = pair // heads, pair % heads
        entries = [picks[b, h, c] for c in range(columns)]
        for c in range(columns):
            fresh = entries[c] >= 0
            for earlier in range(c):
                fresh = fresh & (entries[c] != entries[earlier])
            block = jnp.maximum(entries[c], 0)
            owner = block // per_device
            rank = used[owner]
            slot = owner * CAP + rank
            slot_of[pair * columns + c] = jnp.where(fresh, slot, -1)

            @pl.when(fresh)
            def _():
                used[owner] = rank + 1
                asked[slot] = pair
                code[slot] = block % per_device * heads + h

        return 0

    lax.fori_loop(0, blocks * heads, one_pair, 0)
    lane = lax.broadcasted_iota(jnp.int32, (1, 128), 1)

    def one_owner(d, _):
        meta[d] = jnp.where(lane == 0, code[d * CAP], code[d * CAP + 1])
        return 0

    lax.fori_loop(0, owners, one_owner, 0)


def plan(block_picks, owners):
    blocks, heads, columns = block_picks.shape
    return pl.pallas_call(
        functools.partial(plan_kernel, blocks),
        out_shape=(
            jax.ShapeDtypeStruct((owners * CAP,), jnp.int32),
            jax.ShapeDtypeStruct((blocks * heads * columns,), jnp.int32),
            jax.ShapeDtypeStruct((owners, 1, 128), jnp.int32),
        ),
        in_specs=[pl.BlockSpec(memory_space=pltpu.SMEM)],
        out_specs=(
            pl.BlockSpec(memory_space=pltpu.SMEM),
            pl.BlockSpec(memory_space=pltpu.SMEM),
            pl.BlockSpec(memory_space=pltpu.VMEM),
        ),
        scratch_shapes=[
            pltpu.SMEM((owners,), jnp.int32),
            pltpu.SMEM((owners * CAP,), jnp.int32),
        ],
    )(block_picks)


def tile_partial(query, key, value_t, causal):
    scale = query.shape[-1] ** (-0.5) * LOG2E
    scores = lax.dot_general(
        key, query, (((1,), (1,)), ((), ())), preferred_element_type=jnp.float32
    )
    if causal:
        key_at = lax.broadcasted_iota(jnp.int32, scores.shape, 0)
        query_at = lax.broadcasted_iota(jnp.int32, scores.shape, 1)
        scores = jnp.where(key_at <= query_at, scores, -1e30)
    top = jnp.max(scores, axis=0, keepdims=True)
    shifted = jnp.exp2((scores - top) * scale)
    total = jnp.sum(shifted, axis=0, keepdims=True)
    part = jnp.dot(value_t, shifted.astype(jnp.bfloat16), preferred_element_type=jnp.float32)
    return part.astype(jnp.bfloat16), jnp.concatenate([top * scale, total], axis=0)


def main_kernel(
    rings,
    asked,
    slot_of,
    meta,
    q_ref,
    k_ref,
    v_ref,
    w_hbm,
    out_ref,
    q_tiles,
    k_tiles,
    v_tiles,
    own_part,
    own_stat,
    meta_in,
    meta_sm,
    q_buf,
    part_buf,
    stat_buf,
    gathered,
    total,
    w_ref,
    meta_s,
    meta_r,
    q_s,
    q_r,
    part_s,
    part_r,
    stat_s,
    stat_r,
    local_sem,
    ring_s,
    ring_r,
    mate_s,
    mate_r,
):
    ny, nz = rings
    count = ny * nz
    pairs, rows, width = q_tiles.shape
    heads = q_ref.shape[1] // width
    blocks = pairs // heads
    columns = slot_of.shape[0] // pairs
    groups = gathered.shape[0]
    me = lax.axis_index("seq")
    y, z = me // nz, me % nz
    head_at = lax.axis_index("head")
    mate = head_at + 1 - 2 * (head_at % 2)
    right = (head_at + 2) % groups
    left = (head_at + groups - 2) % groups
    across = (head_at + 4) % groups

    def shift_of(j):
        i = j // ny
        half = (i + 1) // 2
        dz = (nz // 2 + half * (1 - 2 * (i % 2)) + nz) % nz
        return j % ny, dz

    def target(j):
        dy, dz = shift_of(j)
        return (y + dy) % ny * nz + (z + dz) % nz

    def source(j):
        dy, dz = shift_of(j)
        return (y + ny - dy) % ny * nz + (z + nz - dz) % nz

    def each(body):
        def step(j, carry):
            body(j)
            return carry

        lax.fori_loop(0, count, step, 0)

    def meta_copy(d):
        return pltpu.make_async_remote_copy(
            src_ref=meta.at[d], dst_ref=meta_in.at[me], send_sem=meta_s.at[d],
            recv_sem=meta_r.at[me], device_id={"seq": d}, device_id_type=MESH)

    def q_copy(d):
        return pltpu.make_async_remote_copy(
            src_ref=q_buf.at[pl.ds(d * CAP, CAP)], dst_ref=q_buf.at[pl.ds(me * CAP, CAP)],
            send_sem=q_s.at[d], recv_sem=q_r.at[me], device_id={"seq": d}, device_id_type=MESH)

    def part_copy(d):
        return pltpu.make_async_remote_copy(
            src_ref=part_buf.at[pl.ds(d * CAP, CAP)], dst_ref=part_buf.at[pl.ds(me * CAP, CAP)],
            send_sem=part_s.at[d], recv_sem=part_r.at[me], device_id={"seq": d},
            device_id_type=MESH)

    def stat_copy(d):
        return pltpu.make_async_remote_copy(
            src_ref=stat_buf.at[pl.ds(d * CAP, CAP)], dst_ref=stat_buf.at[pl.ds(me * CAP, CAP)],
            send_sem=stat_s.at[d], recv_sem=stat_r.at[me], device_id={"seq": d},
            device_id_type=MESH)

    def arrival(buf, d, sem):
        here = buf.at[pl.ds(d * CAP, CAP)]
        return pltpu.make_async_remote_copy(
            src_ref=here, dst_ref=here, send_sem=sem.at[d], recv_sem=sem.at[d],
            device_id={"seq": d}, device_id_type=MESH)

    meta_in[...] = jnp.zeros_like(meta_in)
    barrier = pltpu.get_barrier_semaphore()

    def greet(j):
        d = target(j)

        @pl.when(d != me)
        def _():
            pl.semaphore_signal(barrier, inc=1, device_id={"seq": d}, device_id_type=MESH)

    each(greet)
    for other in (mate, right, left):
        pl.semaphore_signal(barrier, inc=1, device_id={"head": other}, device_id_type=MESH)

    w_copy = pltpu.make_async_copy(w_hbm, w_ref, local_sem.at[0])
    w_copy.start()
    for b in range(blocks):
        for h in range(heads):
            q_tiles[b * heads + h] = q_ref[b * rows:(b + 1) * rows, h * width:(h + 1) * width]

    def stage(j):
        d = target(j)

        @pl.when(d < me)
        def _():
            for s in range(CAP):
                q_buf[d * CAP + s] = q_tiles[asked[d * CAP + s]]

    each(stage)
    pl.semaphore_wait(barrier, count + 2)

    def send(j):
        d = target(j)

        @pl.when(d < me)
        def _():
            meta_copy(d).start()
            q_copy(d).start()

    each(send)
    for b in range(blocks):
        for h in range(heads):
            p = b * heads + h
            k_tiles[p] = k_ref[b * rows:(b + 1) * rows, h * width:(h + 1) * width]
            v_tiles[p] = v_ref[b * rows:(b + 1) * rows, h * width:(h + 1) * width].T

    def own(p, carry):
        own_part[p], own_stat[p] = tile_partial(q_tiles[p], k_tiles[p], v_tiles[p], True)
        return carry

    lax.fori_loop(0, pairs, own, 0)

    def meta_wait(j):
        d = source(j)

        @pl.when(d > me)
        def _():
            pltpu.make_async_remote_copy(
                src_ref=meta_in.at[d], dst_ref=meta_in.at[d], send_sem=meta_s.at[d],
                recv_sem=meta_r.at[d], device_id={"seq": d}, device_id_type=MESH).wait_recv()

    each(meta_wait)
    meta_copy_in = pltpu.make_async_copy(meta_in, meta_sm, local_sem.at[1])
    meta_copy_in.start()
    meta_copy_in.wait()

    def serve(j):
        d = source(j)

        @pl.when(d > me)
        def _():
            arrival(q_buf, d, q_r).wait_recv()
            for s in range(CAP):
                i = d * CAP + s
                code = meta_sm[d, 0, s]
                part_buf[i], stat_buf[i] = tile_partial(
                    q_buf[i], k_tiles[code], v_tiles[code], False)
            part_copy(d).start()
            stat_copy(d).start()

    each(serve)

    def collect(j):
        d = target(j)

        @pl.when(d < me)
        def _():
            arrival(part_buf, d, part_r).wait_recv()
            arrival(stat_buf, d, stat_r).wait_recv()

    each(collect)

    def merge(p, carry):
        stats = [own_stat[p]]
        used = [None]
        slots = [None]
        for c in range(columns):
            slot = slot_of[p * columns + c]
            used.append(slot >= 0)
            slots.append(jnp.maximum(slot, 0))
            stats.append(stat_buf[slots[-1]])
        tops = [stats[0][:1]] + [
            jnp.where(used[i], stats[i][:1], -1e30) for i in range(1, columns + 1)]
        largest = functools.reduce(jnp.maximum, tops)
        factor = jnp.exp2(tops[0] - largest)
        numer = factor * own_part[p].astype(jnp.float32)
        denom = factor * stats[0][1:]
        for i in range(1, columns + 1):
            factor = jnp.exp2(tops[i] - largest)
            numer += jnp.where(used[i], factor * part_buf[slots[i]].astype(jnp.float32), 0.0)
            denom += jnp.where(used[i], factor * stats[i][1:], 0.0)
        gathered[head_at, p] = (numer / denom).T.astype(jnp.bfloat16)
        return carry

    def unit(g, b):
        return gathered.at[g, pl.ds(b * heads, heads)]

    def hop(g, b, to, k):
        return pltpu.make_async_remote_copy(
            src_ref=unit(g, b), dst_ref=unit(g, b), send_sem=ring_s.at[k],
            recv_sem=ring_r.at[k], device_id={"head": to}, device_id_type=MESH)

    def pass_over(g, b, k):
        return pltpu.make_async_remote_copy(
            src_ref=unit(g, b), dst_ref=unit(g, b), send_sem=mate_s.at[k],
            recv_sem=mate_r.at[k], device_id={"head": mate}, device_id_type=MESH)

    def project(g, b):
        tiles = jnp.concatenate([gathered[g, b * heads + h] for h in range(heads)], axis=1)
        depth = heads * width
        rows_of = pl.ds(b * rows, rows)
        weight = w_ref[pl.ds(pl.multiple_of(g * depth, depth), depth), :]
        total[rows_of, :] += jnp.dot(tiles, weight, preferred_element_type=jnp.float32)

    total[...] = jnp.zeros_like(total)
    sends = []

    def start(copy):
        copy.start()
        sends.append(copy)

    lax.fori_loop(0, heads, merge, 0)
    start(hop(head_at, 0, right, 0))
    start(pass_over(head_at, 0, 0))
    lax.fori_loop(heads, 2 * heads, merge, 0)
    start(hop(head_at, 1, left, 1))
    start(hop(head_at, 1, right, 2))
    start(hop(head_at, 0, left, 3))
    start(pass_over(head_at, 1, 1))
    w_copy.wait()
    project(head_at, 0)
    project(head_at, 1)
    for b in range(2):
        pass_over(mate, b, b).wait_recv()
        project(mate, b)
    plan_in = [
        (left, 0, right, 0, 4),
        (right, 1, left, 1, 5),
        (left, 1, None, 2, None),
        (right, 0, None, 3, None),
        (across, 0, None, 4, None),
        (across, 1, None, 5, None),
    ]
    flip = 1 - 2 * (head_at % 2)
    for n, (g, b, onward, k, k_next) in enumerate(plan_in):
        hop(g, b, right, k).wait_recv()
        if onward is not None:
            start(hop(g, b, onward, k_next))
        start(pass_over(g, b, 2 + n))
        project(g, b)
        pass_over(g + flip, b, 2 + n).wait_recv()
        project(g + flip, b)
    out_ref[...] = total[...].astype(out_ref.dtype)

    def drain(j):
        d = target(j)

        @pl.when(d < me)
        def _():
            meta_copy(d).wait_send()
            q_copy(d).wait_send()

        @pl.when(d > me)
        def _():
            part_copy(d).wait_send()
            stat_copy(d).wait_send()

    each(drain)
    for copy in sends:
        copy.wait_send()


def attend_and_project(asked, slot_of, meta, query_rows, key_rows, value_rows, out_weight, count,
                       groups, heads):
    tok_rows, feature = query_rows.shape
    width = feature // heads
    pairs = slot_of.shape[0] // 4
    rows = tok_rows * heads // pairs
    slots = count * CAP
    vmem = pl.BlockSpec(memory_space=pltpu.VMEM)
    smem = pl.BlockSpec(memory_space=pltpu.SMEM)
    dma = pltpu.SemaphoreType.DMA
    bf16, f32, i32 = jnp.bfloat16, jnp.float32, jnp.int32
    return pl.pallas_call(
        functools.partial(main_kernel, RINGS[count]),
        out_shape=jax.ShapeDtypeStruct((tok_rows, out_weight.shape[1]), bf16),
        in_specs=[smem, smem, vmem, vmem, vmem, vmem, pl.BlockSpec(memory_space=pl.ANY)],
        out_specs=vmem,
        scratch_shapes=[
            pltpu.VMEM((pairs, rows, width), bf16),
            pltpu.VMEM((pairs, rows, width), bf16),
            pltpu.VMEM((pairs, width, rows), bf16),
            pltpu.VMEM((pairs, width, rows), bf16),
            pltpu.VMEM((pairs, 2, rows), f32),
            pltpu.VMEM((count, 1, 128), i32),
            pltpu.SMEM((count, 1, 128), i32),
            pltpu.VMEM((slots, rows, width), bf16),
            pltpu.VMEM((slots, width, rows), bf16),
            pltpu.VMEM((slots, 2, rows), f32),
            pltpu.VMEM((groups, pairs, rows, width), bf16),
            pltpu.VMEM((tok_rows, out_weight.shape[1]), f32),
            pltpu.VMEM(out_weight.shape, bf16),
        ] + [dma((count,)) for _ in range(8)] + [dma((2,)), dma((6,)), dma((6,)), dma((8,)),
                                                 dma((8,))],
        compiler_params=pltpu.CompilerParams(
            collective_id=0, has_side_effects=True, vmem_limit_bytes=60 * 1024 * 1024),
    )(asked, slot_of, meta, query_rows, key_rows, value_rows, out_weight)


def solution(mesh):
    count, groups = mesh.shape["seq"], mesh.shape["head"]

    def body(query_rows, key_rows, value_rows, block_picks, out_weight):
        asked, slot_of, meta = plan(block_picks, count)
        return attend_and_project(asked, slot_of, meta, query_rows, key_rows, value_rows,
                                  out_weight, count, groups, block_picks.shape[1])

    return jax.shard_map(
        body,
        mesh=mesh,
        in_specs=(
            P("seq", "head"),
            P("seq", "head"),
            P("seq", "head"),
            P("seq", "head", None),
            P(None, "head"),
        ),
        out_specs=P("seq", "head"),
        check_vma=False,
    )
```

time: 602 us -> 431 us (0.72)
  Pallas kernels: 0 us -> 429 us
  waiting for transfers between devices: 416 us -> 0 us
  matrix products: 57.1 us -> 0 us
  blocking collectives: 37.8 us -> 0 us
  local copies, waits for them, and re-layouts: 35.7 us -> 2.26 us
  other arithmetic: 29.6 us -> 0 us
  between operations: 13.7 us -> 0.02 us
  starting transfers between devices: 9.26 us -> 0 us
    pallas_call x0 -> x2, Pallas kernels: none -> 429 us  [the longest x1 426 us: attend_and_project(): pl.pallas_call(functools.partial(main_kernel, RINGS[count]), out_shape=ja...]
    all_to_all x1 -> x0, waiting for transfers between devices: 357 us -> none  [body(): lax.all_to_all(outgoing, SEQ, split_axis=0, concat_axis=0, tiled=True)]
    all_gather x1 -> x0, waiting for transfers between devices: 59.5 us -> none  [body(): lax.all_gather(attended, 'head', axis=1, tiled=True)]
    dot_general x7 -> x0, matrix products: 57.1 us -> none  [the longest x3 25.1 us: tile_partial(): jnp.einsum('nqk,nkd->nqd', weights, value_tile, preferred_element_type=jn...]
    all_gather x2 -> x0, blocking collectives: 37.8 us -> none  [all_blocks(): tiles = lax.all_gather(tiles, axes[k])]
    reduce_sum x6 -> x0, other arithmetic: 25.8 us -> none  [the longest x3 18.8 us: tile_partial(): totals = jnp.sum(shifted, axis=-1)]
    gather x2 -> x0, local copies, waits for them, and re-layouts: 18.1 us -> none  [the longest x1 10.7 us: body(): arrived.reshape((seq_count * capacity,) + stacked.shape[1:])[slot_index]]
    all_to_all x1 -> x0, starting transfers between devices: 9.04 us -> none  [body(): lax.all_to_all(outgoing, SEQ, split_axis=0, concat_axis=0, tiled=True)]
  transfers between devices with their start and end apart: 2 -> 0, of which waited for: 2 -> 0; matrix products, arithmetic and copies ran while one was open for 1% -> 0% of each run, Pallas kernels for 0% -> 0%
where the time goes in v1:
time: 431 us
  Pallas kernels  429 us (100%)
    pallas_call x1, Pallas kernels, attend_and_project(): pl.pallas_call(functools.partial(main_kernel, RINGS[count]), out_shape=ja...  426 us

profile of v1, /device:TPU:104, one launch (start us, length us, event | category | flops | bytes accessed | tf_op | source)
XLA Modules:
  0.0 431.0 jit_solution(17707886174928091593)
XLA Ops:
  0.0 2.6 shard_map.55
  2.6 426.1 %shard_map.56 = bf16[1024,512]{1,0:T(8,128)(2,1)} custom-call(s32[64]{0:T(128)} %get-tuple-element.8.asked, s32[32]{0:T(128)} %get-tuple-element.9.slot_of, s32[32,1,128]{2,1,0:T(1,128)} %get-tuple-element.10.meta, bf16[1024,512]{1,0:T(8,128)(2,1)} %q_ref.1, bf16[1024,512]{1,0:T(8,128)(2,1)} %k_ref.1, bf16[1024,512]{1,0:T(8,128)(2,1)} %v_ref.1, ...), custom_call_target="tpu_custom_call" | custom-call | tf_op jit(solution)/shard_map/pallas_call | solution.py:405
  428.7 2.3 copy.7

commit v2 on v1

v2 whole, which is shorter than its diff:
```python
import functools

import jax
import jax.numpy as jnp
from jax import lax
from jax.experimental import pallas as pl
from jax.experimental.pallas import tpu as pltpu
from jax.sharding import PartitionSpec as P

CAP = 2
RINGS = {32: (4, 8)}
LOG2E = 1.4426950408889634
MESH = pl.DeviceIdType.MESH


def plan_kernel(ring, per_device, picks, slot_of, requests, used):
    blocks, heads, columns = picks.shape
    owners = used.shape[0]
    rows_of_owners = requests.shape[0]

    def clear_owner(d, _):
        used[d] = 0
        return 0

    def clear_request(i, _):
        for row in range(rows_of_owners):
            requests[row, i] = 0
        return 0

    lax.fori_loop(0, owners, clear_owner, 0)
    lax.fori_loop(0, 2 * ring * CAP, clear_request, 0)

    def one_pair(pair, _):
        b, h = pair // heads, pair % heads
        entries = [picks[b, h, c] for c in range(columns)]
        for c in range(columns):
            fresh = entries[c] >= 0
            for earlier in range(c):
                fresh = fresh & (entries[c] != entries[earlier])
            block = jnp.maximum(entries[c], 0)
            owner = block // per_device
            rank = used[owner]
            slot_of[pair * columns + c] = jnp.where(fresh, owner * CAP + rank, -1)

            @pl.when(fresh)
            def _():
                used[owner] = rank + 1
                at = owner % ring * CAP + rank
                requests[owner // ring, at] = block % per_device * heads + h
                requests[owner // ring, ring * CAP + at] = pair

        return 0

    lax.fori_loop(0, blocks * heads, one_pair, 0)


def plan(block_picks, rings):
    blocks, heads, columns = block_picks.shape
    ny, nz = rings
    smem = pl.BlockSpec(memory_space=pltpu.SMEM)
    return pl.pallas_call(
        functools.partial(plan_kernel, nz, blocks),
        out_shape=(
            jax.ShapeDtypeStruct((blocks * heads * columns,), jnp.int32),
            jax.ShapeDtypeStruct((ny, 128), jnp.int32),
        ),
        in_specs=[smem],
        out_specs=(smem, smem),
        scratch_shapes=[pltpu.SMEM((ny * nz,), jnp.int32)],
    )(block_picks)


def tile_partial(query, key, value_t, causal):
    scale = query.shape[-1] ** (-0.5) * LOG2E
    scores = lax.dot_general(
        key, query, (((1,), (1,)), ((), ())), preferred_element_type=jnp.float32
    )
    if causal:
        key_at = lax.broadcasted_iota(jnp.int32, scores.shape, 0)
        query_at = lax.broadcasted_iota(jnp.int32, scores.shape, 1)
        scores = jnp.where(key_at <= query_at, scores, -1e30)
    top = jnp.max(scores, axis=0, keepdims=True)
    shifted = jnp.exp2((scores - top) * scale)
    total = jnp.sum(shifted, axis=0, keepdims=True)
    part = jnp.dot(value_t, shifted.astype(jnp.bfloat16), preferred_element_type=jnp.float32)
    return part.astype(jnp.bfloat16), jnp.concatenate([top * scale, total], axis=0)


def main_kernel(
    rings,
    slot_of,
    requests,
    q_ref,
    k_ref,
    v_ref,
    w_hbm,
    out_ref,
    queries,
    own_part,
    own_stat,
    asks,
    asks_sm,
    part_buf,
    stat_buf,
    gathered,
    total,
    w_ref,
    ask_s,
    ask_r,
    q_s,
    q_r,
    part_s,
    part_r,
    stat_s,
    stat_r,
    key_s,
    key_r,
    value_s,
    value_r,
    local_sem,
    ring_s,
    ring_r,
    mate_s,
    mate_r,
    *chunks,
):
    ny, nz = rings
    _, pairs, rows, width = queries.shape
    heads = q_ref.shape[1] // width
    blocks = pairs // heads
    columns = slot_of.shape[0] // pairs
    groups = gathered.shape[0]
    half = nz // 2
    keys, values_t = chunks[:nz], chunks[nz:]
    held = [[0] + [way * (half - 1) + step for step in range(1, half)] + [nz - 1]
            for way in (0, 1)]
    me = lax.axis_index("seq")
    y, z = me // nz, me % nz
    head_at = lax.axis_index("head")
    mate = head_at + 1 - 2 * (head_at % 2)
    right = (head_at + 2) % groups
    left = (head_at + groups - 2) % groups
    across = (head_at + 4) % groups

    def remote(src, dst, send_sem, recv_sem, to):
        return pltpu.make_async_remote_copy(
            src_ref=src, dst_ref=dst, send_sem=send_sem, recv_sem=recv_sem, device_id=to,
            device_id_type=MESH)

    def along_y(row):
        return {"seq": row * nz + z}

    def ask_copy(row):
        return remote(requests.at[row], asks.at[y], ask_s.at[row], ask_r.at[y], along_y(row))

    def query_copy(row):
        return remote(queries.at[y], queries.at[y], q_s.at[row], q_r.at[y], along_y(row))

    def part_copy(row, at):
        src = part_buf.at[pl.ds((row * nz + at) * CAP, CAP)]
        dst = part_buf.at[pl.ds((y * nz + at) * CAP, CAP)]
        return remote(src, dst, part_s.at[row, at], part_r.at[y, at], along_y(row))

    def stat_copy(row, at):
        src = stat_buf.at[pl.ds((row * nz + at) * CAP, CAP)]
        dst = stat_buf.at[pl.ds((y * nz + at) * CAP, CAP)]
        return remote(src, dst, stat_s.at[row, at], stat_r.at[y, at], along_y(row))

    def ring_copy(bufs, sems, way, step):
        turn = 1 - 2 * way
        to = {"seq": y * nz + (z + nz + turn) % nz}
        return remote(bufs[held[way][step]], bufs[held[way][step + 1]], sems[0].at[way, step],
                      sems[1].at[way, step], to)

    def key_copy(way, step):
        return ring_copy(keys, (key_s, key_r), way, step)

    def value_copy(way, step):
        return ring_copy(values_t, (value_s, value_r), way, step)

    def from_below(body):
        def step(row, carry):
            @pl.when(row < y)
            def _():
                body(row)

            return carry

        lax.fori_loop(0, ny, step, 0)

    def from_above(body):
        def step(row, carry):
            @pl.when(row > y)
            def _():
                body(row)

            return carry

        lax.fori_loop(0, ny, step, 0)

    asks[...] = jnp.zeros_like(asks)
    asks[y] = requests[y]
    barrier = pltpu.get_barrier_semaphore()
    for step in range(1, ny):
        pl.semaphore_signal(barrier, inc=1, device_id=along_y((y + step) % ny),
                            device_id_type=MESH)
    for step in (1, nz - 1):
        pl.semaphore_signal(barrier, inc=1, device_id={"seq": y * nz + (z + step) % nz},
                            device_id_type=MESH)
    for other in (mate, right, left):
        pl.semaphore_signal(barrier, inc=1, device_id={"head": other}, device_id_type=MESH)

    w_copy = pltpu.make_async_copy(w_hbm, w_ref, local_sem.at[0])
    w_copy.start()

    def tile(ref, b, h):
        return ref[b * rows:(b + 1) * rows, h * width:(h + 1) * width]

    for b in range(blocks):
        for h in range(heads):
            keys[0][b * heads + h] = tile(k_ref, b, h)
            queries[y, b * heads + h] = tile(q_ref, b, h)
    pl.semaphore_wait(barrier, ny - 1 + 2 + 3)
    from_below(lambda row: ask_copy(row).start())
    key_copy(0, 0).start()
    key_copy(1, 0).start()
    from_below(lambda row: query_copy(row).start())
    for b in range(blocks):
        for h in range(heads):
            values_t[0][b * heads + h] = tile(v_ref, b, h).T
    value_copy(0, 0).start()
    value_copy(1, 0).start()

    def own(p, carry):
        own_part[p], own_stat[p] = tile_partial(
            queries[y, p], keys[0][p], values_t[0][p], True)
        return carry

    lax.fori_loop(0, pairs, own, 0)
    from_above(lambda row: remote(
        requests.at[row], asks.at[row], ask_s.at[row], ask_r.at[row], along_y(row)).wait_recv())
    ask_copy_in = pltpu.make_async_copy(asks, asks_sm, local_sem.at[1])
    ask_copy_in.start()
    ask_copy_in.wait()

    def serve_row(row, at, n):
        for s in range(CAP):
            code = asks_sm[row, 0, at * CAP + s]
            pair = asks_sm[row, 0, (nz + at) * CAP + s]
            i = (row * nz + at) * CAP + s
            part_buf[i], stat_buf[i] = tile_partial(
                queries[row, pair], keys[n][code], values_t[n][code], False)

    def serve(at, n):
        def one(row, carry):
            @pl.when((row > y) | ((row == y) & (at < z)))
            def _():
                serve_row(row, at, n)

            @pl.when(row > y)
            def _():
                part_copy(row, at).start()
                stat_copy(row, at).start()

            return carry

        lax.fori_loop(0, ny, one, 0)

    for step in range(1, half):
        for copy_of, last_way in ((key_copy, 0), (value_copy, 1)):
            for way in (0, 1):
                copy_of(way, step - 1).wait_recv()
                if step < half - 1 or way == last_way:
                    copy_of(way, step).start()
        if step == 1:
            from_above(lambda row: remote(
                queries.at[row], queries.at[row], q_s.at[row], q_r.at[row],
                along_y(row)).wait_recv())
            serve(z, 0)
        serve((z + nz - step) % nz, held[0][step])
        serve((z + step) % nz, held[1][step])
    key_copy(0, half - 1).wait_recv()
    value_copy(1, half - 1).wait_recv()
    serve((z + half) % nz, nz - 1)

    def collect(row):
        def one(at, carry):
            here = pl.ds((row * nz + at) * CAP, CAP)
            remote(part_buf.at[here], part_buf.at[here], part_s.at[row, at], part_r.at[row, at],
                   along_y(row)).wait_recv()
            remote(stat_buf.at[here], stat_buf.at[here], stat_s.at[row, at], stat_r.at[row, at],
                   along_y(row)).wait_recv()
            return carry

        lax.fori_loop(0, nz, one, 0)

    from_below(collect)

    def merge(p, carry):
        stats = [own_stat[p]]
        used = [None]
        slots = [None]
        for c in range(columns):
            slot = slot_of[p * columns + c]
            used.append(slot >= 0)
            slots.append(jnp.maximum(slot, 0))
            stats.append(stat_buf[slots[-1]])
        tops = [stats[0][:1]] + [
            jnp.where(used[i], stats[i][:1], -1e30) for i in range(1, columns + 1)]
        largest = functools.reduce(jnp.maximum, tops)
        factor = jnp.exp2(tops[0] - largest)
        numer = factor * own_part[p].astype(jnp.float32)
        denom = factor * stats[0][1:]
        for i in range(1, columns + 1):
            factor = jnp.exp2(tops[i] - largest)
            numer += jnp.where(used[i], factor * part_buf[slots[i]].astype(jnp.float32), 0.0)
            denom += jnp.where(used[i], factor * stats[i][1:], 0.0)
        gathered[head_at, p] = (numer / denom).T.astype(jnp.bfloat16)
        return carry

    def unit(g, b):
        return gathered.at[g, pl.ds(b * heads, heads)]

    def hop(g, b, to, k):
        return pltpu.make_async_remote_copy(
            src_ref=unit(g, b), dst_ref=unit(g, b), send_sem=ring_s.at[k],
            recv_sem=ring_r.at[k], device_id={"head": to}, device_id_type=MESH)

    def pass_over(g, b, k):
        return pltpu.make_async_remote_copy(
            src_ref=unit(g, b), dst_ref=unit(g, b), send_sem=mate_s.at[k],
            recv_sem=mate_r.at[k], device_id={"head": mate}, device_id_type=MESH)

    def project(g, b):
        tiles = jnp.concatenate([gathered[g, b * heads + h] for h in range(heads)], axis=1)
        depth = heads * width
        rows_of = pl.ds(b * rows, rows)
        weight = w_ref[pl.ds(pl.multiple_of(g * depth, depth), depth), :]
        total[rows_of, :] += jnp.dot(tiles, weight, preferred_element_type=jnp.float32)

    total[...] = jnp.zeros_like(total)
    sends = []

    def start(copy):
        copy.start()
        sends.append(copy)

    lax.fori_loop(0, heads, merge, 0)
    start(hop(head_at, 0, right, 0))
    start(pass_over(head_at, 0, 0))
    lax.fori_loop(heads, 2 * heads, merge, 0)
    start(hop(head_at, 1, left, 1))
    start(hop(head_at, 1, right, 2))
    start(hop(head_at, 0, left, 3))
    start(pass_over(head_at, 1, 1))
    w_copy.wait()
    project(head_at, 0)
    project(head_at, 1)
    for b in range(2):
        pass_over(mate, b, b).wait_recv()
        project(mate, b)
    plan_in = [
        (left, 0, right, 0, 4),
        (right, 1, left, 1, 5),
        (left, 1, None, 2, None),
        (right, 0, None, 3, None),
        (across, 0, None, 4, None),
        (across, 1, None, 5, None),
    ]
    flip = 1 - 2 * (head_at % 2)
    for n, (g, b, onward, k, k_next) in enumerate(plan_in):
        hop(g, b, right, k).wait_recv()
        if onward is not None:
            start(hop(g, b, onward, k_next))
        start(pass_over(g, b, 2 + n))
        project(g, b)
        pass_over(g + flip, b, 2 + n).wait_recv()
        project(g + flip, b)
    out_ref[...] = total[...].astype(out_ref.dtype)

    def drain_below(row):
        ask_copy(row).wait_send()
        query_copy(row).wait_send()

    def drain_above(row):
        def one(at, carry):
            part_copy(row, at).wait_send()
            stat_copy(row, at).wait_send()
            return carry

        lax.fori_loop(0, nz, one, 0)

    from_below(drain_below)
    from_above(drain_above)
    for way in (0, 1):
        for step in range(half):
            if step < half - 1 or way == 0:
                key_copy(way, step).wait_send()
            if step < half - 1 or way == 1:
                value_copy(way, step).wait_send()
    for copy in sends:
        copy.wait_send()


def attend_and_project(slot_of, requests, query_rows, key_rows, value_rows, out_weight, rings,
                       groups, heads, pairs):
    ny, nz = rings
    tok_rows, feature = query_rows.shape
    width = feature // heads
    rows = tok_rows * heads // pairs
    slots = ny * nz * CAP
    vmem = pl.BlockSpec(memory_space=pltpu.VMEM)
    smem = pl.BlockSpec(memory_space=pltpu.SMEM)
    dma = pltpu.SemaphoreType.DMA
    bf16, f32, i32 = jnp.bfloat16, jnp.float32, jnp.int32
    return pl.pallas_call(
        functools.partial(main_kernel, rings),
        out_shape=jax.ShapeDtypeStruct((tok_rows, out_weight.shape[1]), bf16),
        in_specs=[smem, vmem, vmem, vmem, vmem, pl.BlockSpec(memory_space=pl.ANY)],
        out_specs=vmem,
        scratch_shapes=[
            pltpu.VMEM((ny, pairs, rows, width), bf16),
            pltpu.VMEM((pairs, width, rows), bf16),
            pltpu.VMEM((pairs, 2, rows), f32),
            pltpu.VMEM((ny, 1, 128), i32),
            pltpu.SMEM((ny, 1, 128), i32),
            pltpu.VMEM((slots, width, rows), bf16),
            pltpu.VMEM((slots, 2, rows), f32),
            pltpu.VMEM((groups, pairs, rows, width), bf16),
            pltpu.VMEM((tok_rows, out_weight.shape[1]), f32),
            pltpu.VMEM(out_weight.shape, bf16),
        ]
        + [dma((ny,)) for _ in range(4)]
        + [dma((ny, nz)) for _ in range(4)]
        + [dma((2, nz // 2)) for _ in range(4)]
        + [dma((2,)), dma((6,)), dma((6,)), dma((8,)), dma((8,))]
        + [pltpu.VMEM((pairs, rows, width), bf16) for _ in range(nz)]
        + [pltpu.VMEM((pairs, width, rows), bf16) for _ in range(nz)],
        compiler_params=pltpu.CompilerParams(
            collective_id=0, has_side_effects=True, vmem_limit_bytes=60 * 1024 * 1024),
    )(slot_of, requests, query_rows, key_rows, value_rows, out_weight)


def solution(mesh):
    rings, groups = RINGS[mesh.shape["seq"]], mesh.shape["head"]

    def body(query_rows, key_rows, value_rows, block_picks, out_weight):
        blocks, heads, _ = block_picks.shape
        slot_of, requests = plan(block_picks, rings)
        return attend_and_project(slot_of, requests[:, None], query_rows, key_rows, value_rows,
                                  out_weight, rings, groups, heads, blocks * heads)

    return jax.shard_map(
        body,
        mesh=mesh,
        in_specs=(
            P("seq", "head"),
            P("seq", "head"),
            P("seq", "head"),
            P("seq", "head", None),
            P(None, "head"),
        ),
        out_specs=P("seq", "head"),
        check_vma=False,
    )
```

time: 431 us -> 234 us (0.54)
  the two profiles are of different devices: /device:TPU:104 before, /device:TPU:24 now
where the time goes in v2:
time: 234 us
  Pallas kernels  232 us (99%)
    pallas_call x1, Pallas kernels, attend_and_project(): pl.pallas_call(functools.partial(main_kernel, rings), out_shape=jax.Shape...  230 us

profile of v2, /device:TPU:24, one launch (start us, length us, event | category | flops | bytes accessed | tf_op | source)
XLA Modules:
  0.0 234.3 jit_solution(12785999342402728113)
XLA Ops:
  0.0 2.4 %shard_map.55 = (s32[32]{0:T(128)}, s32[4,128]{1,0:T(4,128)}) custom-call(s32[2,4,4]{2,1,0:T(4,128)} %picks.1), custom_call_target="tpu_custom_call" | custom-call | tf_op jit(solution)/shard_map/pallas_call | solution.py:61
  2.4 229.6 %shard_map.56 = bf16[1024,512]{1,0:T(8,128)(2,1)} custom-call(s32[32]{0:T(128)} %get-tuple-element.7.slot_of, s32[4,1,128]{2,1,0:T(1,128)} %bitcast.1, bf16[1024,512]{1,0:T(8,128)(2,1)} %q_ref.1, bf16[1024,512]{1,0:T(8,128)(2,1)} %k_ref.1, bf16[1024,512]{1,0:T(8,128)(2,1)} %v_ref.1, bf16[4096,512]{1,0:T(8,128)(2,1)} %w_hbm.1), custom_call_target="tpu_custom_call" | custom-call | tf_op jit(solution)/shard_map/pallas_call | solution.py:416
  232.1 2.3 copy.7

commit v3 on v2

--- a/solution.py
+++ b/solution.py
@@ -122,6 +122,8 @@
     ring_r,
     mate_s,
     mate_r,
+    q_go,
+    ring_go,
     *chunks,
 ):
     ny, nz = rings
@@ -141,6 +143,8 @@
     right = (head_at + 2) % groups
     left = (head_at + groups - 2) % groups
     across = (head_at + 4) % groups
+    leads = head_at % 2 == 0
+    follows = head_at % 2 == 1
 
     def remote(src, dst, send_sem, recv_sem, to):
         return pltpu.make_async_remote_copy(
@@ -221,15 +225,31 @@
             keys[0][b * heads + h] = tile(k_ref, b, h)
             queries[y, b * heads + h] = tile(q_ref, b, h)
     pl.semaphore_wait(barrier, ny - 1 + 2 + 3)
+    def start_queries():
+        from_below(lambda row: query_copy(row).start())
+
+    def start_ring():
+        for way in (0, 1):
+            key_copy(way, 0).start()
+        for way in (0, 1):
+            value_copy(way, 0).start()
+
     from_below(lambda row: ask_copy(row).start())
-    key_copy(0, 0).start()
-    key_copy(1, 0).start()
-    from_below(lambda row: query_copy(row).start())
+
+    @pl.when(leads)
+    def _():
+        key_copy(0, 0).start()
+        key_copy(1, 0).start()
+        start_queries()
+
     for b in range(blocks):
         for h in range(heads):
             values_t[0][b * heads + h] = tile(v_ref, b, h).T
-    value_copy(0, 0).start()
-    value_copy(1, 0).start()
+
+    @pl.when(leads)
+    def _():
+        value_copy(0, 0).start()
+        value_copy(1, 0).start()
 
     def own(p, carry):
         own_part[p], own_stat[p] = tile_partial(
@@ -237,6 +257,16 @@
         return carry
 
     lax.fori_loop(0, pairs, own, 0)
+    total[...] = jnp.zeros_like(total)
+    w_copy.wait()
+
+    @pl.when(follows)
+    def _():
+        pl.semaphore_wait(q_go, 1)
+        start_queries()
+        pl.semaphore_wait(ring_go, 1)
+        start_ring()
+
     from_above(lambda row: remote(
         requests.at[row], asks.at[row], ask_s.at[row], ask_r.at[row], along_y(row)).wait_recv())
     ask_copy_in = pltpu.make_async_copy(asks, asks_sm, local_sem.at[1])
@@ -252,7 +282,9 @@
                 queries[row, pair], keys[n][code], values_t[n][code], False)
 
     def serve(at, n):
-        def one(row, carry):
+        def one(i, carry):
+            row = ny - 1 - i
+
             @pl.when((row > y) | ((row == y) & (at < z)))
             def _():
                 serve_row(row, at, n)
@@ -273,12 +305,60 @@
                 if step < half - 1 or way == last_way:
                     copy_of(way, step).start()
         if step == 1:
+            @pl.when(leads)
+            def _():
+                pl.semaphore_signal(q_go, inc=1, device_id={"head": mate}, device_id_type=MESH)
+
             from_above(lambda row: remote(
                 queries.at[row], queries.at[row], q_s.at[row], q_r.at[row],
                 along_y(row)).wait_recv())
             serve(z, 0)
+        if step == half - 1:
+            @pl.when(leads)
+            def _():
+                pl.semaphore_signal(ring_go, inc=1, device_id={"head": mate}, device_id_type=MESH)
+
         serve((z + nz - step) % nz, held[0][step])
         serve((z + step) % nz, held[1][step])
+    def unit(g, b):
+        return gathered.at[g, pl.ds(b * heads, heads)]
+
+    def hop(g, b, to, k):
+        return pltpu.make_async_remote_copy(
+            src_ref=unit(g, b), dst_ref=unit(g, b), send_sem=ring_s.at[k],
+            recv_sem=ring_r.at[k], device_id={"head": to}, device_id_type=MESH)
+
+    def pass_over(g, b, k):
+        return pltpu.make_async_remote_copy(
+            src_ref=unit(g, b), dst_ref=unit(g, b), send_sem=mate_s.at[k],
+            recv_sem=mate_r.at[k], device_id={"head": mate}, device_id_type=MESH)
+
+    def project(g, b):
+        tiles = jnp.concatenate([gathered[g, b * heads + h] for h in range(heads)], axis=1)
+        depth = heads * width
+        rows_of = pl.ds(b * rows, rows)
+        weight = w_ref[pl.ds(pl.multiple_of(g * depth, depth), depth), :]
+        total[rows_of, :] += jnp.dot(tiles, weight, preferred_element_type=jnp.float32)
+
+    arrivals = [
+        (left, 0, right, 0, 4),
+        (right, 1, left, 1, 5),
+        (left, 1, None, 2, None),
+        (right, 0, None, 3, None),
+        (across, 0, None, 4, None),
+        (across, 1, None, 5, None),
+    ]
+    flip = 1 - 2 * (head_at % 2)
+
+    def project_mates():
+        for b in range(2):
+            pass_over(mate, b, b).wait_recv()
+            project(mate, b)
+        for n, (g, b, _, _, _) in enumerate(arrivals):
+            pass_over(g + flip, b, 2 + n).wait_recv()
+            project(g + flip, b)
+
+    pl.when(follows)(project_mates)
     key_copy(0, half - 1).wait_recv()
     value_copy(1, half - 1).wait_recv()
     serve((z + half) % nz, nz - 1)
@@ -318,27 +398,6 @@
         gathered[head_at, p] = (numer / denom).T.astype(jnp.bfloat16)
         return carry
 
-    def unit(g, b):
-        return gathered.at[g, pl.ds(b * heads, heads)]
-
-    def hop(g, b, to, k):
-        return pltpu.make_async_remote_copy(
-            src_ref=unit(g, b), dst_ref=unit(g, b), send_sem=ring_s.at[k],
-            recv_sem=ring_r.at[k], device_id={"head": to}, device_id_type=MESH)
-
-    def pass_over(g, b, k):
-        return pltpu.make_async_remote_copy(
-            src_ref=unit(g, b), dst_ref=unit(g, b), send_sem=mate_s.at[k],
-            recv_sem=mate_r.at[k], device_id={"head": mate}, device_id_type=MESH)
-
-    def project(g, b):
-        tiles = jnp.concatenate([gathered[g, b * heads + h] for h in range(heads)], axis=1)
-        depth = heads * width
-        rows_of = pl.ds(b * rows, rows)
-        weight = w_ref[pl.ds(pl.multiple_of(g * depth, depth), depth), :]
-        total[rows_of, :] += jnp.dot(tiles, weight, preferred_element_type=jnp.float32)
-
-    total[...] = jnp.zeros_like(total)
     sends = []
 
     def start(copy):
@@ -353,29 +412,15 @@
     start(hop(head_at, 1, right, 2))
     start(hop(head_at, 0, left, 3))
     start(pass_over(head_at, 1, 1))
-    w_copy.wait()
     project(head_at, 0)
     project(head_at, 1)
-    for b in range(2):
-        pass_over(mate, b, b).wait_recv()
-        project(mate, b)
-    plan_in = [
-        (left, 0, right, 0, 4),
-        (right, 1, left, 1, 5),
-        (left, 1, None, 2, None),
-        (right, 0, None, 3, None),
-        (across, 0, None, 4, None),
-        (across, 1, None, 5, None),
-    ]
-    flip = 1 - 2 * (head_at % 2)
-    for n, (g, b, onward, k, k_next) in enumerate(plan_in):
+    for n, (g, b, onward, k, k_next) in enumerate(arrivals):
         hop(g, b, right, k).wait_recv()
         if onward is not None:
             start(hop(g, b, onward, k_next))
         start(pass_over(g, b, 2 + n))
         project(g, b)
-        pass_over(g + flip, b, 2 + n).wait_recv()
-        project(g + flip, b)
+    pl.when(leads)(project_mates)
     out_ref[...] = total[...].astype(out_ref.dtype)
 
     def drain_below(row):
@@ -434,6 +479,7 @@
         + [dma((ny, nz)) for _ in range(4)]
         + [dma((2, nz // 2)) for _ in range(4)]
         + [dma((2,)), dma((6,)), dma((6,)), dma((8,)), dma((8,))]
+        + [pltpu.SemaphoreType.REGULAR] * 2
         + [pltpu.VMEM((pairs, rows, width), bf16) for _ in range(nz)]
         + [pltpu.VMEM((pairs, width, rows), bf16) for _ in range(nz)],
         compiler_params=pltpu.CompilerParams(

time: 234 us -> 214 us (0.915)
  the two profiles are of different devices: /device:TPU:24 before, /device:TPU:104 now
where the time goes in v3:
time: 214 us; the launch traced here: 212 us
  Pallas kernels  210 us (98%)
  local copies, waits for them, and re-layouts  2.26 us (1%)
    pallas_call x1, Pallas kernels, attend_and_project(): pl.pallas_call(functools.partial(main_kernel, rings), out_shape=jax.Shape...  208 us

profile of v3, /device:TPU:104, one launch (start us, length us, event | category | flops | bytes accessed | tf_op | source)
XLA Modules:
  0.0 212.4 jit_solution(11723085950176506383)
XLA Ops:
  0.0 2.4 %shard_map.55 = (s32[32]{0:T(128)}, s32[4,128]{1,0:T(4,128)}) custom-call(s32[2,4,4]{2,1,0:T(4,128)} %picks.1), custom_call_target="tpu_custom_call" | custom-call | tf_op jit(solution)/shard_map/pallas_call | solution.py:61
  2.4 207.7 %shard_map.56 = bf16[1024,512]{1,0:T(8,128)(2,1)} custom-call(s32[32]{0:T(128)} %get-tuple-element.7.slot_of, s32[4,1,128]{2,1,0:T(1,128)} %bitcast.1, bf16[1024,512]{1,0:T(8,128)(2,1)} %q_ref.1, bf16[1024,512]{1,0:T(8,128)(2,1)} %k_ref.1, bf16[1024,512]{1,0:T(8,128)(2,1)} %v_ref.1, bf16[4096,512]{1,0:T(8,128)(2,1)} %w_hbm.1), custom_call_target="tpu_custom_call" | custom-call | tf_op jit(solution)/shard_map/pallas_call | solution.py:461
  210.1 2.3 %copy.7 = bf16[1024,512]{1,0:T(8,128)(2,1)} copy(bf16[1024,512]{1,0:T(8,128)(2,1)} %shard_map.56) | data formatting | bytes 2097152

commit v4 on v3

v4 whole, which is shorter than its diff:
```python
import functools

import jax
import jax.numpy as jnp
from jax import lax
from jax.experimental import pallas as pl
from jax.experimental.pallas import tpu as pltpu
from jax.sharding import PartitionSpec as P

CAP = 2
RINGS = {32: (4, 8)}
LOG2E = 1.4426950408889634
MESH = pl.DeviceIdType.MESH


def tile_partial(query, key, value_t, causal):
    scale = query.shape[-1] ** (-0.5) * LOG2E
    scores = lax.dot_general(
        key, query, (((1,), (1,)), ((), ())), preferred_element_type=jnp.float32
    )
    if causal:
        key_at = lax.broadcasted_iota(jnp.int32, scores.shape, 0)
        query_at = lax.broadcasted_iota(jnp.int32, scores.shape, 1)
        scores = jnp.where(key_at <= query_at, scores, -1e30)
    top = jnp.max(scores, axis=0, keepdims=True)
    shifted = jnp.exp2((scores - top) * scale)
    total = jnp.sum(shifted, axis=0, keepdims=True)
    part = jnp.dot(value_t, shifted.astype(jnp.bfloat16), preferred_element_type=jnp.float32)
    return part.astype(jnp.bfloat16), jnp.concatenate([top * scale, total], axis=0)


def main_kernel(
    rings,
    picks,
    q_hbm,
    k_hbm,
    v_hbm,
    w_hbm,
    out_ref,
    queries,
    v_tiles,
    own_part,
    own_stat,
    asks,
    asks_sm,
    part_buf,
    stat_buf,
    gathered,
    total,
    w_ref,
    ask_s,
    ask_r,
    q_s,
    q_r,
    part_s,
    part_r,
    stat_s,
    stat_r,
    key_s,
    key_r,
    value_s,
    value_r,
    local_sem,
    tile_sem,
    ring_s,
    ring_r,
    mate_s,
    mate_r,
    q_go,
    ring_go,
    *chunks,
):
    ny, nz = rings
    _, pairs, rows, width = queries.shape
    blocks, heads, columns = picks.shape
    entries = pairs * columns
    slots = ny * nz * CAP
    groups = gathered.shape[0]
    half = nz // 2
    keys, values_t = chunks[:nz], chunks[nz:]
    held = [[0] + [way * (half - 1) + step for step in range(1, half)] + [nz - 1]
            for way in (0, 1)]
    me = lax.axis_index("seq")
    y, z = me // nz, me % nz
    head_at = lax.axis_index("head")
    mate = head_at + 1 - 2 * (head_at % 2)
    right = (head_at + 2) % groups
    left = (head_at + groups - 2) % groups
    across = (head_at + 4) % groups
    leads = head_at % 2 == 0
    follows = head_at % 2 == 1

    def remote(src, dst, send_sem, recv_sem, to):
        return pltpu.make_async_remote_copy(
            src_ref=src, dst_ref=dst, send_sem=send_sem, recv_sem=recv_sem, device_id=to,
            device_id_type=MESH)

    def along_y(row):
        return {"seq": row * nz + z}

    def ask_copy(row):
        return remote(asks.at[y], asks.at[y], ask_s.at[row], ask_r.at[y], along_y(row))

    def query_copy(row):
        return remote(queries.at[y], queries.at[y], q_s.at[row], q_r.at[y], along_y(row))

    def part_copy(row, at, s):
        n = at * CAP + s
        return remote(part_buf.at[row * nz * CAP + n], part_buf.at[y * nz * CAP + n],
                      part_s.at[row, n], part_r.at[y, n], along_y(row))

    def stat_copy(row, at):
        src = stat_buf.at[pl.ds((row * nz + at) * CAP, CAP)]
        dst = stat_buf.at[pl.ds((y * nz + at) * CAP, CAP)]
        return remote(src, dst, stat_s.at[row, at], stat_r.at[y, at], along_y(row))

    def ring_copy(bufs, sems, way, step):
        turn = 1 - 2 * way
        to = {"seq": y * nz + (z + nz + turn) % nz}
        return remote(bufs[held[way][step]], bufs[held[way][step + 1]], sems[0].at[way, step],
                      sems[1].at[way, step], to)

    def key_copy(way, step):
        return ring_copy(keys, (key_s, key_r), way, step)

    def value_copy(way, step):
        return ring_copy(values_t, (value_s, value_r), way, step)

    def from_below(body):
        def step(row, carry):
            @pl.when(row < y)
            def _():
                body(row)

            return carry

        lax.fori_loop(0, ny, step, 0)

    def from_above(body):
        def step(row, carry):
            @pl.when(row > y)
            def _():
                body(row)

            return carry

        lax.fori_loop(0, ny, step, 0)

    def fetch(kind, p):
        b, h = p // heads, p % heads
        src = (k_hbm, q_hbm, v_hbm)[kind]
        dst = (keys[0], queries.at[y], v_tiles)[kind]
        return pltpu.make_async_copy(
            src.at[pl.ds(b * rows, rows), pl.ds(h * width, width)], dst.at[p],
            tile_sem.at[kind, p])

    asks[...] = jnp.zeros_like(asks)
    barrier = pltpu.get_barrier_semaphore()
    for step in range(1, ny):
        pl.semaphore_signal(barrier, inc=1, device_id=along_y((y + step) % ny),
                            device_id_type=MESH)
    for step in (1, nz - 1):
        pl.semaphore_signal(barrier, inc=1, device_id={"seq": y * nz + (z + step) % nz},
                            device_id_type=MESH)
    for other in (mate, right, left):
        pl.semaphore_signal(barrier, inc=1, device_id={"head": other}, device_id_type=MESH)
    for kind in range(3):
        for p in range(pairs):
            fetch(kind, p).start()
    w_copy = pltpu.make_async_copy(w_hbm, w_ref, local_sem.at[0])
    w_copy.start()

    lane = lax.broadcasted_iota(jnp.int32, (1, 128), 1)

    def owners_of(pair):
        b, h = pair // heads, pair % heads
        named = [picks[b, h, c] for c in range(columns)]
        found = []
        for c in range(columns):
            fresh = named[c] >= 0
            for earlier in range(c):
                fresh = fresh & (named[c] != named[earlier])
            block = jnp.maximum(named[c], 0)
            found.append((jnp.where(fresh, block // blocks, -1), block % blocks * heads + h))
        return found

    def place(pair, carry):
        wanted, used, owner_at = carry
        for c, (owner, code) in enumerate(owners_of(pair)):
            of_owner = lane % slots // CAP == owner
            hit = of_owner & (lane % CAP == used)
            wanted = jnp.where(hit, jnp.where(lane < slots, code, pair), wanted)
            used = jnp.where(of_owner, used + 1, used)
            owner_at = jnp.where(lane == pair * columns + c, owner, owner_at)
        return wanted, used, owner_at

    none = jnp.zeros((1, 128), jnp.int32)
    wanted, _, owner_at = lax.fori_loop(0, pairs, place, (none, none, none - 1))
    asks[y] = wanted

    def rank(pair, earlier):
        for c, (owner, _) in enumerate(owners_of(pair)):
            earlier += jnp.where((owner_at == owner) & (lane > pair * columns + c), 1, 0)
        return earlier

    ranks = lax.fori_loop(0, pairs, rank, none)
    asks[ny] = jnp.where(owner_at >= 0, owner_at * CAP + ranks, -1)
    for p in range(pairs):
        fetch(0, p).wait()
    pl.semaphore_wait(barrier, ny - 1 + 2 + 3)

    def start_queries():
        from_below(lambda row: query_copy(row).start())

    def start_ring():
        for way in (0, 1):
            key_copy(way, 0).start()
        for way in (0, 1):
            value_copy(way, 0).start()

    from_below(lambda row: ask_copy(row).start())

    @pl.when(leads)
    def _():
        key_copy(0, 0).start()
        key_copy(1, 0).start()

    for p in range(pairs):
        fetch(1, p).wait()

    @pl.when(leads)
    def _():
        start_queries()

    for p in range(pairs):
        fetch(2, p).wait()
        values_t[0][p] = v_tiles[p].T

    @pl.when(leads)
    def _():
        value_copy(0, 0).start()
        value_copy(1, 0).start()

    def own(p, carry):
        own_part[p], own_stat[p] = tile_partial(
            queries[y, p], keys[0][p], values_t[0][p], True)
        return carry

    lax.fori_loop(0, pairs, own, 0)
    total[...] = jnp.zeros_like(total)
    w_copy.wait()

    @pl.when(follows)
    def _():
        pl.semaphore_wait(q_go, 1)
        start_queries()
        pl.semaphore_wait(ring_go, 1)
        start_ring()

    from_above(lambda row: remote(
        asks.at[row], asks.at[row], ask_s.at[row], ask_r.at[row], along_y(row)).wait_recv())
    ask_copy_in = pltpu.make_async_copy(asks, asks_sm, local_sem.at[1])
    ask_copy_in.start()
    ask_copy_in.wait()

    def serve_row(row, at, n):
        for s in range(CAP):
            lane_of = (y * nz + at) * CAP + s
            code = asks_sm[row, 0, lane_of]
            pair = asks_sm[row, 0, slots + lane_of]
            i = (row * nz + at) * CAP + s
            part_buf[i], stat_buf[i] = tile_partial(
                queries[row, pair], keys[n][code], values_t[n][code], False)

            @pl.when(row > y)
            def _():
                part_copy(row, at, s).start()

    def serve(at, n):
        def one(i, carry):
            row = ny - 1 - i

            @pl.when((row > y) | ((row == y) & (at < z)))
            def _():
                serve_row(row, at, n)

            @pl.when(row > y)
            def _():
                stat_copy(row, at).start()

            return carry

        lax.fori_loop(0, ny, one, 0)

    for step in range(1, half):
        for copy_of, last_way in ((key_copy, 0), (value_copy, 1)):
            for way in (0, 1):
                copy_of(way, step - 1).wait_recv()
                if step < half - 1 or way == last_way:
                    copy_of(way, step).start()
        if step == 1:
            @pl.when(leads)
            def _():
                pl.semaphore_signal(q_go, inc=1, device_id={"head": mate}, device_id_type=MESH)

            from_above(lambda row: remote(
                queries.at[row], queries.at[row], q_s.at[row], q_r.at[row],
                along_y(row)).wait_recv())
            serve(z, 0)
        if step == half - 2:
            @pl.when(leads)
            def _():
                pl.semaphore_signal(ring_go, inc=1, device_id={"head": mate}, device_id_type=MESH)

        serve((z + nz - step) % nz, held[0][step])
        serve((z + step) % nz, held[1][step])
    parts = 2 * blocks
    tiles_in = pairs // parts

    def unit(g, u):
        return gathered.at[g, pl.ds(u * tiles_in, tiles_in)]

    def hop(g, u, way, k):
        return remote(unit(g, u), unit(g, u), ring_s.at[way, k], ring_r.at[way, k],
                      {"head": (right, left)[way]})

    def pass_over(g, u, k):
        return remote(unit(g, u), unit(g, u), mate_s.at[k], mate_r.at[k], {"head": mate})

    def project(g, u):
        tiles = jnp.concatenate(
            [gathered[g, u * tiles_in + t] for t in range(tiles_in)], axis=1)
        depth = tiles_in * width
        at = pl.multiple_of(g * heads * width + u % 2 * depth, depth)
        rows_of = pl.ds(u // 2 * rows, rows)
        total[rows_of, :] += jnp.dot(
            tiles, w_ref[pl.ds(at, depth), :], preferred_element_type=jnp.float32)

    orders = ((0, 1, 2, 3), (2, 3, 0, 1))
    arrivals = [((left, right)[way], orders[way][k], way, k) for k in range(parts)
                for way in (0, 1)]
    arrivals += [(across, orders[way][k], way, parts + k) for k in (0, 1) for way in (0, 1)]
    flip = 1 - 2 * (head_at % 2)

    def project_mates():
        for u in (0, 2, 1, 3):
            pass_over(mate, u, u).wait_recv()
            project(mate, u)
        for n, (g, u, _, _) in enumerate(arrivals):
            pass_over(g + flip, u, parts + n).wait_recv()
            project(g + flip, u)

    pl.when(follows)(project_mates)
    key_copy(0, half - 1).wait_recv()
    value_copy(1, half - 1).wait_recv()
    serve((z + half) % nz, nz - 1)

    def collect(row):
        def one(n, carry):
            here = part_buf.at[row * nz * CAP + n]
            remote(here, here, part_s.at[row, n], part_r.at[row, n], along_y(row)).wait_recv()
            return carry

        def other(at, carry):
            here = stat_buf.at[pl.ds((row * nz + at) * CAP, CAP)]
            remote(here, here, stat_s.at[row, at], stat_r.at[row, at], along_y(row)).wait_recv()
            return carry

        lax.fori_loop(0, nz * CAP, one, 0)
        lax.fori_loop(0, nz, other, 0)

    from_below(collect)

    def merge(p, carry):
        stats = [own_stat[p]]
        used = [None]
        slots = [None]
        for c in range(columns):
            slot = asks_sm[ny, 0, p * columns + c]
            used.append(slot >= 0)
            slots.append(jnp.maximum(slot, 0))
            stats.append(stat_buf[slots[-1]])
        tops = [stats[0][:1]] + [
            jnp.where(used[i], stats[i][:1], -1e30) for i in range(1, columns + 1)]
        largest = functools.reduce(jnp.maximum, tops)
        factor = jnp.exp2(tops[0] - largest)
        numer = factor * own_part[p].astype(jnp.float32)
        denom = factor * stats[0][1:]
        for i in range(1, columns + 1):
            factor = jnp.exp2(tops[i] - largest)
            numer += jnp.where(used[i], factor * part_buf[slots[i]].astype(jnp.float32), 0.0)
            denom += jnp.where(used[i], factor * stats[i][1:], 0.0)
        gathered[head_at, p] = (numer * (1.0 / denom)).astype(jnp.bfloat16).T
        return carry

    sends = []

    def start(copy):
        copy.start()
        sends.append(copy)

    for u, way in ((0, 0), (2, 1), (1, 0), (3, 1)):
        lax.fori_loop(u * tiles_in, (u + 1) * tiles_in, merge, 0)
        start(hop(head_at, u, way, u % 2))
        start(pass_over(head_at, u, u))
    for u, way in ((2, 0), (0, 1), (3, 0), (1, 1)):
        start(hop(head_at, u, way, 2 + u % 2))
    for u in range(parts):
        project(head_at, u)
    for n, (g, u, way, k) in enumerate(arrivals):
        hop(g, u, way, k).wait_recv()
        if k < 2:
            start(hop(g, u, way, parts + k))
        start(pass_over(g, u, parts + n))
        project(g, u)
    pl.when(leads)(project_mates)
    out_ref[...] = total[...].astype(out_ref.dtype)

    def drain_below(row):
        ask_copy(row).wait_send()
        query_copy(row).wait_send()

    def drain_above(row):
        def one(at, carry):
            for s in range(CAP):
                part_copy(row, at, s).wait_send()
            stat_copy(row, at).wait_send()
            return carry

        lax.fori_loop(0, nz, one, 0)

    from_below(drain_below)
    from_above(drain_above)
    for way in (0, 1):
        for step in range(half):
            if step < half - 1 or way == 0:
                key_copy(way, step).wait_send()
            if step < half - 1 or way == 1:
                value_copy(way, step).wait_send()
    for copy in sends:
        copy.wait_send()


def attend_and_project(picks, query_rows, key_rows, value_rows, out_weight, rings, groups):
    ny, nz = rings
    blocks, heads, _ = picks.shape
    tok_rows, feature = query_rows.shape
    width, rows, pairs = feature // heads, tok_rows // blocks, blocks * heads
    slots = ny * nz * CAP
    hbm = pl.BlockSpec(memory_space=pl.ANY)
    dma = pltpu.SemaphoreType.DMA
    bf16, f32, i32 = jnp.bfloat16, jnp.float32, jnp.int32
    return pl.pallas_call(
        functools.partial(main_kernel, rings),
        out_shape=jax.ShapeDtypeStruct((tok_rows, out_weight.shape[1]), bf16),
        in_specs=[pl.BlockSpec(memory_space=pltpu.SMEM), hbm, hbm, hbm, hbm],
        out_specs=pl.BlockSpec(memory_space=pltpu.VMEM),
        scratch_shapes=[
            pltpu.VMEM((ny, pairs, rows, width), bf16),
            pltpu.VMEM((pairs, rows, width), bf16),
            pltpu.VMEM((pairs, width, rows), bf16),
            pltpu.VMEM((pairs, 2, rows), f32),
            pltpu.VMEM((ny + 1, 1, 128), i32),
            pltpu.SMEM((ny + 1, 1, 128), i32),
            pltpu.VMEM((slots, width, rows), bf16),
            pltpu.VMEM((slots, 2, rows), f32),
            pltpu.VMEM((groups, pairs, rows, width), bf16),
            pltpu.VMEM((tok_rows, out_weight.shape[1]), f32),
            pltpu.VMEM(out_weight.shape, bf16),
        ]
        + [dma((ny,)) for _ in range(4)]
        + [dma((ny, nz * CAP)) for _ in range(2)]
        + [dma((ny, nz)) for _ in range(2)]
        + [dma((2, nz // 2)) for _ in range(4)]
        + [dma((2,)), dma((3, pairs)), dma((2, 6)), dma((2, 6)), dma((16,)), dma((16,))]
        + [pltpu.SemaphoreType.REGULAR] * 2
        + [pltpu.VMEM((pairs, rows, width), bf16) for _ in range(nz)]
        + [pltpu.VMEM((pairs, width, rows), bf16) for _ in range(nz)],
        compiler_params=pltpu.CompilerParams(
            collective_id=0, has_side_effects=True, vmem_limit_bytes=60 * 1024 * 1024),
    )(picks, query_rows, key_rows, value_rows, out_weight)


def solution(mesh):
    rings, groups = RINGS[mesh.shape["seq"]], mesh.shape["head"]

    def body(query_rows, key_rows, value_rows, block_picks, out_weight):
        return attend_and_project(
            block_picks, query_rows, key_rows, value_rows, out_weight, rings, groups)

    return jax.shard_map(
        body,
        mesh=mesh,
        in_specs=(
            P("seq", "head"),
            P("seq", "head"),
            P("seq", "head"),
            P("seq", "head", None),
            P(None, "head"),
        ),
        out_specs=P("seq", "head"),
        check_vma=False,
    )
```

time: 214 us -> 207 us (0.967)
  Pallas kernels: 210 us -> 204 us
    pallas_call x1, Pallas kernels: 208 us -> 204 us  [attend_and_project(): pl.pallas_call(functools.partial(main_kernel, rings), out_shape=jax.Shape...]
    pallas_call x1 -> x0, Pallas kernels: 2.41 us -> none  [plan(): pl.pallas_call(functools.partial(plan_kernel, nz, blocks), out_shape=(jax...]
where the time goes in v4:
time: 207 us; the launch traced here: 206 us
  Pallas kernels  204 us (99%)
  local copies, waits for them, and re-layouts  2.26 us (1%)
    pallas_call x1, Pallas kernels, attend_and_project(): pl.pallas_call(functools.partial(main_kernel, rings), out_shape=jax.Shape...  204 us

profile of v4, /device:TPU:104, one launch (start us, length us, event | category | flops | bytes accessed | tf_op | source)
XLA Modules:
  0.0 206.0 jit_solution(12506003150134296637)
XLA Ops:
  0.0 203.8 %shard_map.55 = bf16[1024,512]{1,0:T(8,128)(2,1)} custom-call(s32[2,4,4]{2,1,0:T(4,128)} %picks.1, bf16[1024,512]{1,0:T(8,128)(2,1)} %q_hbm.1, bf16[1024,512]{1,0:T(8,128)(2,1)} %k_hbm.1, bf16[1024,512]{1,0:T(8,128)(2,1)} %v_hbm.1, bf16[4096,512]{1,0:T(8,128)(2,1)} %w_hbm.1), custom_call_target="tpu_custom_call" | custom-call | tf_op jit(solution)/shard_map/pallas_call | solution.py:453
  203.8 2.3 %copy.7 = bf16[1024,512]{1,0:T(8,128)(2,1)} copy(bf16[1024,512]{1,0:T(8,128)(2,1)} %shard_map.55) | data formatting | bytes 2097152

commit v5 on v4

--- a/solution.py
+++ b/solution.py
@@ -8,6 +8,7 @@
 from jax.sharding import PartitionSpec as P
 
 CAP = 2
+LENT = 2
 RINGS = {32: (4, 8)}
 LOG2E = 1.4426950408889634
 MESH = pl.DeviceIdType.MESH
@@ -68,6 +69,18 @@
     mate_r,
     q_go,
     ring_go,
+    guests,
+    slot_queries,
+    row_ask_s,
+    row_ask_r,
+    slot_q_s,
+    slot_q_r,
+    lend_s,
+    lend_r,
+    guest_s,
+    guest_r,
+    back_s,
+    back_r,
     *chunks,
 ):
     ny, nz = rings
@@ -89,6 +102,10 @@
     across = (head_at + 4) % groups
     leads = head_at % 2 == 0
     follows = head_at % 2 == 1
+    last = ny - 1
+    kept = pairs - LENT
+    in_ring = y < last
+    helps = y == last
 
     def remote(src, dst, send_sem, recv_sem, to):
         return pltpu.make_async_remote_copy(
@@ -114,17 +131,67 @@
         dst = stat_buf.at[pl.ds((y * nz + at) * CAP, CAP)]
         return remote(src, dst, stat_s.at[row, at], stat_r.at[y, at], along_y(row))
 
-    def ring_copy(bufs, sems, way, step):
-        turn = 1 - 2 * way
-        to = {"seq": y * nz + (z + nz + turn) % nz}
-        return remote(bufs[held[way][step]], bufs[held[way][step + 1]], sems[0].at[way, step],
-                      sems[1].at[way, step], to)
+    def along_z(at):
+        return {"seq": y * nz + at}
+
+    def ring_to(way):
+        return along_z((z + nz + 1 - 2 * way) % nz)
 
     def key_copy(way, step):
-        return ring_copy(keys, (key_s, key_r), way, step)
+        here, there = keys[held[way][step]], keys[held[way][step + 1]]
+        span = pl.ds(0, pairs)
+        if step == half - 1:
+            span = (pl.ds(0, pairs - 1), pl.ds(pairs - 1, 1))[way]
+        return remote(here.at[span], there.at[span], key_s.at[way, step], key_r.at[way, step],
+                      ring_to(way))
 
     def value_copy(way, step):
-        return ring_copy(values_t, (value_s, value_r), way, step)
+        here, there = values_t[held[way][step]], values_t[held[way][step + 1]]
+        span = pl.ds(0, kept)
+        return remote(here.at[span], there.at[span], value_s.at[way, step],
+                      value_r.at[way, step], ring_to(way))
+
+    def guest(n, row, first=0, size=LENT):
+        span = pl.ds(row * LENT + first, size)
+        return guests.at[span] if n == 0 else values_t[n].at[span]
+
+    def lend_copy(row):
+        return remote(values_t[0].at[pl.ds(kept, LENT)], guest(0, row), lend_s.at[0],
+                      lend_r.at[row], along_y(last))
+
+    def guest_copy(row, way, step):
+        cut = (0, LENT) if step < half - 1 else (way * (LENT // 2), LENT // 2)
+        return remote(guest(held[way][step], row, *cut), guest(held[way][step + 1], row, *cut),
+                      guest_s.at[row, way, step], guest_r.at[row, way, step], ring_to(way))
+
+    def back_copy(row, n):
+        return remote(guest(n, row), values_t[n].at[pl.ds(kept, LENT)], back_s.at[row, n],
+                      back_r.at[n], along_y(row))
+
+    def row_ask_copy(at):
+        return remote(asks.at[y], asks.at[ny + 1 + z], row_ask_s.at[at], row_ask_r.at[z],
+                      along_z(at))
+
+    def slot_query_copy(at):
+        return remote(slot_queries.at[pl.ds(at * CAP, CAP)],
+                      slot_queries.at[pl.ds(z * CAP, CAP)], slot_q_s.at[at], slot_q_r.at[z],
+                      along_z(at))
+
+    def row_part_copy(at, s):
+        return remote(part_buf.at[(y * nz + at) * CAP + s], part_buf.at[(y * nz + z) * CAP + s],
+                      part_s.at[y, at * CAP + s], part_r.at[y, z * CAP + s], along_z(at))
+
+    def row_stat_copy(at):
+        return remote(stat_buf.at[pl.ds((y * nz + at) * CAP, CAP)],
+                      stat_buf.at[pl.ds((y * nz + z) * CAP, CAP)], stat_s.at[y, at],
+                      stat_r.at[y, z], along_z(at))
+
+    def over(low, high, body):
+        def step(at, carry):
+            body(at)
+            return carry
+
+        lax.fori_loop(low, high, step, 0)
 
     def from_below(body):
         def step(row, carry):
@@ -159,8 +226,8 @@
     for step in range(1, ny):
         pl.semaphore_signal(barrier, inc=1, device_id=along_y((y + step) % ny),
                             device_id_type=MESH)
-    for step in (1, nz - 1):
-        pl.semaphore_signal(barrier, inc=1, device_id={"seq": y * nz + (z + step) % nz},
+    for step in range(1, nz):
+        pl.semaphore_signal(barrier, inc=1, device_id=along_z((z + step) % nz),
                             device_id_type=MESH)
     for other in (mate, right, left):
         pl.semaphore_signal(barrier, inc=1, device_id={"head": other}, device_id_type=MESH)
@@ -207,7 +274,7 @@
     asks[ny] = jnp.where(owner_at >= 0, owner_at * CAP + ranks, -1)
     for p in range(pairs):
         fetch(0, p).wait()
-    pl.semaphore_wait(barrier, ny - 1 + 2 + 3)
+    pl.semaphore_wait(barrier, ny - 1 + nz - 1 + 3)
 
     def start_queries():
         from_below(lambda row: query_copy(row).start())
@@ -220,10 +287,14 @@
 
     from_below(lambda row: ask_copy(row).start())
 
-    @pl.when(leads)
+    @pl.when(leads & in_ring)
     def _():
         key_copy(0, 0).start()
         key_copy(1, 0).start()
+
+    @pl.when(helps)
+    def _():
+        over(0, z, lambda at: row_ask_copy(at).start())
 
     for p in range(pairs):
         fetch(1, p).wait()
@@ -236,10 +307,25 @@
         fetch(2, p).wait()
         values_t[0][p] = v_tiles[p].T
 
-    @pl.when(leads)
+    @pl.when(in_ring)
+    def _():
+        lend_copy(y).start()
+
+    @pl.when(leads & in_ring)
     def _():
         value_copy(0, 0).start()
         value_copy(1, 0).start()
+
+    def begin_guests():
+        def begin(row):
+            remote(guest(0, row), guest(0, row), lend_s.at[0], lend_r.at[row],
+                   along_y(row)).wait_recv()
+            for way in (0, 1):
+                guest_copy(row, way, 0).start()
+
+        over(0, last, begin)
+
+    pl.when(leads & helps)(begin_guests)
 
     def own(p, carry):
         own_part[p], own_stat[p] = tile_partial(
@@ -247,6 +333,14 @@
         return carry
 
     lax.fori_loop(0, pairs, own, 0)
+
+    def greenlight(sem):
+        pl.semaphore_signal(sem, inc=1, device_id={"head": mate}, device_id_type=MESH)
+
+    @pl.when(leads & helps)
+    def _():
+        greenlight(q_go)
+
     total[...] = jnp.zeros_like(total)
     w_copy.wait()
 
@@ -255,10 +349,18 @@
         pl.semaphore_wait(q_go, 1)
         start_queries()
         pl.semaphore_wait(ring_go, 1)
-        start_ring()
+        pl.when(in_ring)(start_ring)
+        pl.when(helps)(begin_guests)
 
     from_above(lambda row: remote(
         asks.at[row], asks.at[row], ask_s.at[row], ask_r.at[row], along_y(row)).wait_recv())
+
+    @pl.when(helps)
+    def _():
+        over(z + 1, nz, lambda at: remote(
+            asks.at[ny + 1 + at], asks.at[ny + 1 + at], row_ask_s.at[at], row_ask_r.at[at],
+            along_z(at)).wait_recv())
+
     ask_copy_in = pltpu.make_async_copy(asks, asks_sm, local_sem.at[1])
     ask_copy_in.start()
     ask_copy_in.wait()
@@ -292,28 +394,84 @@
 
         lax.fori_loop(0, ny, one, 0)
 
-    for step in range(1, half):
-        for copy_of, last_way in ((key_copy, 0), (value_copy, 1)):
+    def take_back(n):
+        here = values_t[n].at[pl.ds(kept, LENT)]
+        remote(here, here, back_s.at[0, n], back_r.at[n], along_y(last)).wait_recv()
+
+    def serve_both(step):
+        for way, at in ((0, (z + nz - step) % nz), (1, (z + step) % nz)):
+            take_back(held[way][step])
+            serve(at, held[way][step])
+
+    @pl.when(in_ring)
+    def _():
+        for step in range(1, half):
+            for copy_of, final in ((key_copy, (0, 1)), (value_copy, (1,))):
+                for way in (0, 1):
+                    copy_of(way, step - 1).wait_recv()
+                    if step < half - 1 or way in final:
+                        copy_of(way, step).start()
+            if step == 1:
+                @pl.when(leads)
+                def _():
+                    greenlight(q_go)
+
+                from_above(lambda row: remote(
+                    queries.at[row], queries.at[row], q_s.at[row], q_r.at[row],
+                    along_y(row)).wait_recv())
+                serve(z, 0)
+            if step == half - 2:
+                @pl.when(leads)
+                def _():
+                    greenlight(ring_go)
+
+            if step > 1:
+                serve_both(step - 1)
+        serve_both(half - 1)
+
+    @pl.when(helps)
+    def _():
+        for step in range(1, half):
+            def onward(row):
+                for way in (0, 1):
+                    guest_copy(row, way, step - 1).wait_recv()
+                    guest_copy(row, way, step).start()
+                    back_copy(row, held[way][step]).start()
+
+            over(0, last, onward)
+
+        def finish(row):
             for way in (0, 1):
-                copy_of(way, step - 1).wait_recv()
-                if step < half - 1 or way == last_way:
-                    copy_of(way, step).start()
-        if step == 1:
-            @pl.when(leads)
-            def _():
-                pl.semaphore_signal(q_go, inc=1, device_id={"head": mate}, device_id_type=MESH)
-
-            from_above(lambda row: remote(
-                queries.at[row], queries.at[row], q_s.at[row], q_r.at[row],
-                along_y(row)).wait_recv())
-            serve(z, 0)
-        if step == half - 2:
-            @pl.when(leads)
-            def _():
-                pl.semaphore_signal(ring_go, inc=1, device_id={"head": mate}, device_id_type=MESH)
-
-        serve((z + nz - step) % nz, held[0][step])
-        serve((z + step) % nz, held[1][step])
+                guest_copy(row, way, half - 1).wait_recv()
+            back_copy(row, nz - 1).start()
+
+        over(0, last, finish)
+
+        @pl.when(leads)
+        def _():
+            greenlight(ring_go)
+
+        def ask_slot(at):
+            for s in range(CAP):
+                lane_of = (y * nz + at) * CAP + s
+                slot_queries[at * CAP + s] = queries[y, asks_sm[y, 0, slots + lane_of]]
+
+        over(0, z, ask_slot)
+        over(0, z, lambda at: slot_query_copy(at).start())
+
+        def serve_slots(at):
+            here = slot_queries.at[pl.ds(at * CAP, CAP)]
+            remote(here, here, slot_q_s.at[at], slot_q_r.at[at], along_z(at)).wait_recv()
+            for s in range(CAP):
+                code = asks_sm[ny + 1 + at, 0, (y * nz + z) * CAP + s]
+                i = (y * nz + at) * CAP + s
+                part_buf[i], stat_buf[i] = tile_partial(
+                    slot_queries[at * CAP + s], keys[0][code], values_t[0][code], False)
+                row_part_copy(at, s).start()
+            row_stat_copy(at).start()
+
+        over(z + 1, nz, serve_slots)
+
     parts = 2 * blocks
     tiles_in = pairs // parts
 
@@ -350,10 +508,13 @@
             pass_over(g + flip, u, parts + n).wait_recv()
             project(g + flip, u)
 
-    pl.when(follows)(project_mates)
-    key_copy(0, half - 1).wait_recv()
-    value_copy(1, half - 1).wait_recv()
-    serve((z + half) % nz, nz - 1)
+    @pl.when(in_ring)
+    def _():
+        key_copy(0, half - 1).wait_recv()
+        key_copy(1, half - 1).wait_recv()
+        take_back(nz - 1)
+        value_copy(1, half - 1).wait_recv()
+        serve((z + half) % nz, nz - 1)
 
     def collect(row):
         def one(n, carry):
@@ -369,7 +530,20 @@
         lax.fori_loop(0, nz * CAP, one, 0)
         lax.fori_loop(0, nz, other, 0)
 
+    pl.when(follows)(project_mates)
     from_below(collect)
+
+    @pl.when(helps)
+    def _():
+        def collect_slots(at):
+            for s in range(CAP):
+                here = part_buf.at[(y * nz + at) * CAP + s]
+                n = at * CAP + s
+                remote(here, here, part_s.at[y, n], part_r.at[y, n], along_z(at)).wait_recv()
+            here = stat_buf.at[pl.ds((y * nz + at) * CAP, CAP)]
+            remote(here, here, stat_s.at[y, at], stat_r.at[y, at], along_z(at)).wait_recv()
+
+        over(0, z, collect_slots)
 
     def merge(p, carry):
         stats = [own_stat[p]]
@@ -431,12 +605,38 @@
 
     from_below(drain_below)
     from_above(drain_above)
-    for way in (0, 1):
-        for step in range(half):
-            if step < half - 1 or way == 0:
+
+    @pl.when(in_ring)
+    def _():
+        lend_copy(y).wait_send()
+        for way in (0, 1):
+            for step in range(half):
                 key_copy(way, step).wait_send()
-            if step < half - 1 or way == 1:
-                value_copy(way, step).wait_send()
+                if step < half - 1 or way == 1:
+                    value_copy(way, step).wait_send()
+
+    @pl.when(helps)
+    def _():
+        def drain_asks(at):
+            row_ask_copy(at).wait_send()
+            slot_query_copy(at).wait_send()
+
+        def drain_parts(at):
+            for s in range(CAP):
+                row_part_copy(at, s).wait_send()
+            row_stat_copy(at).wait_send()
+
+        def drain_guests(row):
+            for way in (0, 1):
+                for step in range(half):
+                    guest_copy(row, way, step).wait_send()
+            for n in range(1, nz):
+                back_copy(row, n).wait_send()
+
+        over(0, z, drain_asks)
+        over(z + 1, nz, drain_parts)
+        over(0, last, drain_guests)
+
     for copy in sends:
         copy.wait_send()
 
@@ -460,8 +660,8 @@
             pltpu.VMEM((pairs, rows, width), bf16),
             pltpu.VMEM((pairs, width, rows), bf16),
             pltpu.VMEM((pairs, 2, rows), f32),
-            pltpu.VMEM((ny + 1, 1, 128), i32),
-            pltpu.SMEM((ny + 1, 1, 128), i32),
+            pltpu.VMEM((ny + 1 + nz, 1, 128), i32),
+            pltpu.SMEM((ny + 1 + nz, 1, 128), i32),
             pltpu.VMEM((slots, width, rows), bf16),
             pltpu.VMEM((slots, 2, rows), f32),
             pltpu.VMEM((groups, pairs, rows, width), bf16),
@@ -474,6 +674,12 @@
         + [dma((2, nz // 2)) for _ in range(4)]
         + [dma((2,)), dma((3, pairs)), dma((2, 6)), dma((2, 6)), dma((16,)), dma((16,))]
         + [pltpu.SemaphoreType.REGULAR] * 2
+        + [pltpu.VMEM(((ny - 1) * LENT, width, rows), bf16),
+           pltpu.VMEM((nz * CAP, rows, width), bf16)]
+        + [dma((nz,)) for _ in range(4)]
+        + [dma((1,)), dma((ny - 1,))]
+        + [dma((ny - 1, 2, nz // 2)) for _ in range(2)]
+        + [dma((ny - 1, nz)), dma((nz,))]
         + [pltpu.VMEM((pairs, rows, width), bf16) for _ in range(nz)]
         + [pltpu.VMEM((pairs, width, rows), bf16) for _ in range(nz)],
         compiler_params=pltpu.CompilerParams(

time: 207 us -> 202 us (0.976); the launches traced: 206 us -> 199 us
  Pallas kernels: 204 us -> 197 us
    pallas_call x1, Pallas kernels: 204 us -> 197 us  [attend_and_project(): pl.pallas_call(functools.partial(main_kernel, rings), out_shape=jax.Shape...]
where the time goes in v5:
time: 202 us; the launch traced here: 199 us
  Pallas kernels  197 us (98%)
  local copies, waits for them, and re-layouts  2.26 us (1%)
    pallas_call x1, Pallas kernels, attend_and_project(): pl.pallas_call(functools.partial(main_kernel, rings), out_shape=jax.Shape...  197 us

profile of v5, /device:TPU:104, one launch (start us, length us, event | category | flops | bytes accessed | tf_op | source)
XLA Modules:
  0.0 198.8 jit_solution(15111230264760069613)
XLA Ops:
  0.0 196.5 %shard_map.55 = bf16[1024,512]{1,0:T(8,128)(2,1)} custom-call(s32[2,4,4]{2,1,0:T(4,128)} %picks.1, bf16[1024,512]{1,0:T(8,128)(2,1)} %q_hbm.1, bf16[1024,512]{1,0:T(8,128)(2,1)} %k_hbm.1, bf16[1024,512]{1,0:T(8,128)(2,1)} %v_hbm.1, bf16[4096,512]{1,0:T(8,128)(2,1)} %w_hbm.1), custom_call_target="tpu_custom_call" | custom-call | tf_op jit(solution)/shard_map/pallas_call | solution.py:653
  196.5 2.3 %copy.7 = bf16[1024,512]{1,0:T(8,128)(2,1)} copy(bf16[1024,512]{1,0:T(8,128)(2,1)} %shard_map.55) | data formatting | bytes 2097152

commit v6 on v5

--- a/solution.py
+++ b/solution.py
@@ -431,6 +431,15 @@
 
     @pl.when(helps)
     def _():
+        def ask_slot(at):
+            for s in range(CAP):
+                lane_of = (y * nz + at) * CAP + s
+                slot_queries[at * CAP + s] = queries[y, asks_sm[y, 0, slots + lane_of]]
+
+        def ask_slots():
+            over(0, z, ask_slot)
+            over(0, z, lambda at: slot_query_copy(at).start())
+
         for step in range(1, half):
             def onward(row):
                 for way in (0, 1):
@@ -439,6 +448,8 @@
                     back_copy(row, held[way][step]).start()
 
             over(0, last, onward)
+            if step == 1:
+                pl.when(follows)(ask_slots)
 
         def finish(row):
             for way in (0, 1):
@@ -451,13 +462,7 @@
         def _():
             greenlight(ring_go)
 
-        def ask_slot(at):
-            for s in range(CAP):
-                lane_of = (y * nz + at) * CAP + s
-                slot_queries[at * CAP + s] = queries[y, asks_sm[y, 0, slots + lane_of]]
-
-        over(0, z, ask_slot)
-        over(0, z, lambda at: slot_query_copy(at).start())
+        pl.when(leads)(ask_slots)
 
         def serve_slots(at):
             here = slot_queries.at[pl.ds(at * CAP, CAP)]

time: 202 us -> 202 us (level)
  no operation moved by 1% of the time
where the time goes in v6:
time: 202 us; the launch traced here: 199 us
  Pallas kernels  197 us (98%)
  local copies, waits for them, and re-layouts  2.26 us (1%)
    pallas_call x1, Pallas kernels, attend_and_project(): pl.pallas_call(functools.partial(main_kernel, rings), out_shape=jax.Shape...  197 us

profile of v6, /device:TPU:104, one launch (start us, length us, event | category | flops | bytes accessed | tf_op | source)
XLA Modules:
  0.0 198.8 jit_solution(6969745811427639684)
XLA Ops:
  0.0 196.5 %shard_map.55 = bf16[1024,512]{1,0:T(8,128)(2,1)} custom-call(s32[2,4,4]{2,1,0:T(4,128)} %picks.1, bf16[1024,512]{1,0:T(8,128)(2,1)} %q_hbm.1, bf16[1024,512]{1,0:T(8,128)(2,1)} %k_hbm.1, bf16[1024,512]{1,0:T(8,128)(2,1)} %v_hbm.1, bf16[4096,512]{1,0:T(8,128)(2,1)} %w_hbm.1), custom_call_target="tpu_custom_call" | custom-call | tf_op jit(solution)/shard_map/pallas_call | solution.py:658
  196.5 2.3 %copy.7 = bf16[1024,512]{1,0:T(8,128)(2,1)} copy(bf16[1024,512]{1,0:T(8,128)(2,1)} %shard_map.55) | data formatting | bytes 2097152
